TPU v7x, 32 devices: a whole 2x2x4 slice. The times are simulated.
32 devices in a mesh: mod: 2 (over y), dp: 16 (over z, x, core).
Axes of the slice: x: 2, y: 2, z: 4, core: 2. Of those that a mesh axis runs over, the one named last changes fastest.
Arguments:
- image_pooled: bfloat16 [640, 1024], P('dp'), may hold values from -6 to 6
- text_pooled: bfloat16 [640, 768], P('dp'), may hold values from -6 to 6
- image_gain: float32 [1024], replicated, may hold values from 0.25 to 1.75
- text_gain: float32 [768], replicated, may hold values from 0.25 to 1.75
- image_proj: bfloat16 [1024, 768], replicated, may hold values from -0.1875 to 0.1875
- text_proj: bfloat16 [768, 768], replicated, may hold values from -0.21875 to 0.21875
- logit_scale: float32 [1], replicated, may hold values from 10 to 100
- pair_index: int32 [2, 640], P('mod', 'dp'), may hold values from 0 to 639, as said below
Outputs:
- loss_value: float32 [], replicated
- embed_grad: float32 [2, 640, 768], P('mod', 'dp')
Inputs may be any that keep to these rules, and one draw needn't show every extreme that they name: `pair_index`: row 0 is a permutation of 0 to 639 and row 1 is its inverse permutation.
All inputs are finite; a program needn't handle non-finite values.
Results may differ from a plain program's by a relative error of at most 0.0041.
Values may be sent and summed in bfloat16 or wider, within the bound.
No kernel may reach another device: no remote copies, remote signals or barrier semaphores. Data moves between devices by JAX's collectives and lax.ppermute only.
A program may use at most 128 MiB of HBM per device.

v0:
```python
import jax
import jax.numpy as jnp
from jax import lax
from jax.sharding import PartitionSpec as P


def from_partner(x, axis, bit):
    return lax.ppermute(x, axis, [(i, i ^ 1 << bit) for i in range(lax.axis_size(axis))])


def normalize_project(pooled, gain, weight):
    features = pooled.astype(jnp.float32)
    centered = features - jnp.mean(features, axis=-1, keepdims=True)
    variance = jnp.mean(centered * centered, axis=-1, keepdims=True)
    normalized = (centered * lax.rsqrt(variance + 1e-05) * gain).astype(jnp.bfloat16)
    return jnp.dot(normalized, weight, preferred_element_type=jnp.float32)


def unitize(embedded):
    lengths = jnp.sqrt(jnp.sum(embedded * embedded, axis=-1, keepdims=True) + 1e-06)
    return (embedded / lengths, lengths)


def similarity(left_rows, right_rows, scale_value):
    return scale_value * lax.dot_general(
        left_rows, right_rows, (((1,), (1,)), ((), ())), preferred_element_type=jnp.float32
    )


def local(
    image_pooled, text_pooled, image_gain, text_gain, image_proj, text_proj, logit_scale, pair_index
):
    module_index = lax.axis_index("mod")
    embedded = lax.cond(
        module_index == 0,
        lambda: normalize_project(image_pooled, image_gain, image_proj),
        lambda: normalize_project(text_pooled, text_gain, text_proj),
    )
    unit_rows, lengths = unitize(embedded)
    unit_half = unit_rows.astype(jnp.bfloat16)
    mirror_rows = from_partner(unit_half, "mod", 0)
    scale_value = logit_scale[0]
    row_count = unit_rows.shape[0]
    batch_total = row_count * lax.axis_size("dp")
    gathered = lax.all_gather(mirror_rows, "dp", axis=0, tiled=True)
    scores = similarity(unit_half, gathered, scale_value)
    running_max = jnp.max(scores, axis=1)
    own_lse = running_max + jnp.log(jnp.sum(jnp.exp(scores - running_max[:, None]), axis=1))
    columns = lax.broadcasted_iota(jnp.int32, (row_count, batch_total), 1)
    matched = columns == pair_index[0][:, None]
    diagonal = jnp.sum(jnp.where(matched, scores, 0.0), axis=1)
    every_lse, every_diag = (
        lax.all_gather(own_lse, ("mod", "dp"), axis=0, tiled=True),
        lax.all_gather(diagonal, ("mod", "dp"), axis=0, tiled=True),
    )
    other_lse = lax.dynamic_slice_in_dim(every_lse, (1 - module_index) * batch_total, batch_total)
    loss_value = (jnp.sum(every_lse) - jnp.sum(every_diag)) / (2.0 * batch_total)
    pair_weight = (
        jnp.exp(scores - own_lse[:, None])
        + jnp.exp(scores - other_lse[None, :])
        - 2.0 * matched.astype(jnp.float32)
    ).astype(jnp.bfloat16)
    unit_grad = (
        scale_value
        / (2.0 * batch_total)
        * jnp.dot(pair_weight, gathered, preferred_element_type=jnp.float32)
    )
    embed_grad = (
        unit_grad - unit_rows * jnp.sum(unit_rows * unit_grad, axis=-1, keepdims=True)
    ) / lengths
    return (loss_value, embed_grad[None])


def solution(mesh):
    in_specs = (P("dp", None), P("dp", None), P(), P(), P(), P(), P(), P("mod", "dp"))
    out_specs = (P(), P("mod", "dp", None))
    return jax.shard_map(local, mesh=mesh, in_specs=in_specs, out_specs=out_specs, check_vma=False)
```

profile of v0, /device:TPU:0, one launch (start us, length us, event | category | flops | bytes accessed | tf_op | source)
XLA Modules:
  0.0 78.1 jit_solution(6129029324738736359)
XLA Ops:
  0.6 4.1 %conditional.1 = (f32[40,768]{1,0:T(8,128)S(1)}, f32[40,1]{0,1:T(1,128)S(1)}) conditional(s32[]{:T(128)} %convert_element_type.22, (bf16[40,768]{1,0:T(8,128)(2,1)}, f32[768]{0:T(1024)}, bf16[768,768]{1,0:T(8,128)(2,1)}) %tuple.18, (bf16[40,1024]{1,0:T(8,128)(2,1)}, f32[1024]{0:T(1024)}, bf16[1024,768]{1,0:T(8,128)(2,1)}) %tuple.19), branch_computations={%region_0.4_spmd, %region_4.8_spmd} | conditional | flops 63426560 | bytes 1947216 | solution.py:34
  0.7 1.0 %convert_reduce_fusion.1 = f32[40]{0:T(128)S(1)} fusion(bf16[40,1024]{1,0:T(8,128)(2,1)} %get-tuple-element.35), kind=kLoop, calls=%fused_computation.15 | loop fusion | flops 81880 | bytes 82080 | tf_op jit(solution)/shard_map/cond/branch_1_fun/reduce_sum | solution.py:13
  1.7 1.1 %fusion.12 = f32[40]{0:T(128)S(1)} fusion(bf16[40,1024]{1,0:T(8,128)(2,1)} %get-tuple-element.35, f32[40]{0:T(128)S(1)} %broadcast_multiply_fusion.1), kind=kLoop, calls=%fused_computation.18 | loop fusion | flops 163800 | bytes 82240 | tf_op jit(solution)/shard_map/cond/branch_1_fun/reduce_sum | solution.py:14
  2.8 2.0 %multiply_reduce_fusion.1 = (f32[40]{0:T(128)S(1)}, f32[40,768]{1,0:T(8,128)S(1)}) fusion(bf16[1024,768]{1,0:T(8,128)(2,1)} %get-tuple-element.37, bf16[40,1024]{1,0:T(8,128)(2,1)} %get-tuple-element.35, f32[1024]{0:T(1024)} %get-tuple-element.36, f32[40]{0:T(128)S(1)} %add_rsqrt_fusion.1, f32[40]{0:T(128)S(1)} %broadcast_multiply_fusion.1), kind=kOutput, calls=%fused_computation.21 | convolution fusion | flops 63180760 | bytes 1782240 | tf_op jit(solution)/shard_map/cond/branch_1_fun/dot_general | solution.py:16
  4.8 0.0 copy-start
  4.8 0.1 fusion.27
  4.9 2.7 %collective-permute-start = (bf16[40,768]{1,0:T(8,128)(2,1)S(1)}, bf16[40,768]{1,0:T(8,128)(2,1)S(1)}, u32[]{:S(2)}, u32[]{:S(2)}) collective-permute-start(bf16[40,768]{1,0:T(8,128)(2,1)S(1)} %fusion.27), channel_id=1, source_target_pairs={{0,16},{16,0},{1,17},{17,1},{2,18},{18,2},{3,19},{19,3},{4,20},{20... | collective-permute-start | bytes 184328 | tf_op jit(solution)/shard_map/ppermute | solution.py:8
  8.3 1.5 %collective-permute-done = bf16[40,768]{1,0:T(8,128)(2,1)S(1)} collective-permute-done((bf16[40,768]{1,0:T(8,128)(2,1)S(1)}, bf16[40,768]{1,0:T(8,128)(2,1)S(1)}, u32[]{:S(2)}, u32[]{:S(2)}) %collective-permute-start) | collective-permute-done | bytes 61472 | tf_op jit(solution)/shard_map/ppermute | solution.py:8
  9.8 25.3 %all_gather.9 = bf16[640,768]{1,0:T(8,128)(2,1)S(1)} all-gather(bf16[40,768]{1,0:T(8,128)(2,1)S(1)} %collective-permute-done), channel_id=1, replica_groups=mesh['mod'=2,'dp'=16] {'dp'}, dimensions={0}, use_global_device_ids=true | all-gather | bytes 1044480 | tf_op jit(solution)/shard_map/all_gather | solution.py:45
  35.1 0.5 fusion.29
  35.6 0.0 copy-done
  35.6 0.2 select_reduce_fusion
  35.8 0.3 dynamic-update-slice.1
  36.1 0.1 fusion.28
  36.2 37.0 %all-reduce.2 = (f32[1280]{0:T(1024)S(1)}, f32[1280]{0:T(1024)S(1)}) all-reduce(f32[1280]{0:T(1024)S(1)} %get-tuple-element.42, f32[1280]{0:T(1024)S(1)} %dynamic-update-slice.1), channel_id=1, replica_groups=mesh['mod'=2,'dp'=16] {'mod','dp'}, use_global_device_ids=true, to_apply=%add | all-reduce | flops 2560 | bytes 20480
  73.2 0.6 reduce_sum.102
  73.8 0.6 reduce_sum.104
  75.7 0.1 dynamic_slice.3
  75.8 0.4 multiply_reduce_fusion.2
  76.2 0.8 divide_bitcast_fusion
  (5 shorter events, 0.0 us)
Async XLA Ops:
  4.8 30.9 %copy-start = (s32[1,40]{1,0:T(1,128)S(1)}, s32[1,40]{1,0:T(1,128)}, u32[]{:S(2)}) copy-start(s32[1,40]{1,0:T(1,128)} %param.17) | copy-start | bytes 484
  4.9 4.9 %collective-permute-start = (bf16[40,768]{1,0:T(8,128)(2,1)S(1)}, bf16[40,768]{1,0:T(8,128)(2,1)S(1)}, u32[]{:S(2)}, u32[]{:S(2)}) collective-permute-start(bf16[40,768]{1,0:T(8,128)(2,1)S(1)} %fusion.27), channel_id=1, source_target_pairs={{0,16},{16,0},{1,17},{17,1},{2,18},{18,2},{3,19},{19,3},{4,20},{20... | collective-permute-start | bytes 184328 | tf_op jit(solution)/shard_map/ppermute | solution.py:8
where the time goes:
time: 79 us; the launch traced here: 78.1 us
  blocking collectives  62.3 us (79%)
  other arithmetic  4.46 us (6%)
  between operations  3.76 us (5%)
  matrix products  2.94 us (4%)
  starting transfers between devices  2.74 us (3%)
  waiting for transfers between devices  1.55 us (2%)
    unnamed x1, blocking collectives  37 us
    all_gather x1, blocking collectives, local(): gathered = lax.all_gather(mirror_rows, 'dp', axis=0, tiled=True)  25.3 us
    ppermute x1, starting transfers between devices, from_partner(): lax.ppermute(x, axis, [(i, i ^ 1 << bit) for i in range(lax.axis_size(axi...  2.74 us
    dot_general x1, matrix products, normalize_project(): return jnp.dot(normalized, weight, preferred_element_type=jnp.float32)  2 us
  transfers between devices with their start and end apart: 1, of which 1 were waited for; matrix products, arithmetic and copies ran while one was open for 0% of the time, Pallas kernels for 0%

commit v1 on v0

--- a/solution.py
+++ b/solution.py
@@ -1,7 +1,32 @@
 import jax
 import jax.numpy as jnp
+import numpy as np
 from jax import lax
 from jax.sharding import PartitionSpec as P
+
+LANES = 128
+SCORE_BYTES = 2**24
+
+
+def closed_path(mesh):
+    places = [getattr(d, "coords", None) for d in mesh.devices[0]]
+    natural = list(range(len(places)))
+    if any(p is None for p in places):
+        return natural
+    chips = {}
+    for i, p in enumerate(places):
+        chips.setdefault(tuple(p), []).append(i)
+    span = [sorted({c[k] for c in chips}) for k in range(3)]
+    wide = [k for k in range(3) if len(span[k]) > 1]
+    if len(wide) != 2 or len(chips) != len(span[wide[0]]) * len(span[wide[1]]):
+        return natural
+    short, long = sorted(wide, key=lambda k: len(span[k]))
+    if len(span[short]) != 2:
+        return natural
+    by = {(c[short], c[long]): v for c, v in chips.items()}
+    there = [by[span[short][0], z] for z in span[long]]
+    back = [by[span[short][1], z] for z in reversed(span[long])]
+    return [i for cores in there + back for i in cores]
 
 
 def from_partner(x, axis, bit):
@@ -27,7 +52,69 @@
     )
 
 
-def local(
+def log_sum_exp(scores, axis):
+    top = jnp.max(scores, axis=axis)
+    return top + jnp.log(jnp.sum(jnp.exp(scores - jnp.expand_dims(top, axis)), axis=axis))
+
+
+def gather_both(
+    order, image_pooled, text_pooled, image_gain, text_gain, image_proj, text_proj, logit_scale, pair_index
+):
+    is_image = lax.axis_index("mod") == 0
+    image_unit, image_len = unitize(normalize_project(image_pooled, image_gain, image_proj))
+    text_unit, text_len = unitize(normalize_project(text_pooled, text_gain, text_proj))
+    unit_rows = jnp.where(is_image, image_unit, text_unit)
+    other_rows = jnp.where(is_image, text_unit, image_unit)
+    lengths = jnp.where(is_image, image_len, text_len)
+    scale_value = logit_scale[0]
+    row_count, width = unit_rows.shape
+    batch_total = row_count * lax.axis_size("dp")
+    pairs = pair_index[0][:, None]
+    lane = lax.broadcasted_iota(jnp.int32, (row_count, LANES), 1)
+    digits = jnp.where(lane == 0, pairs // LANES, jnp.where(lane == 1, pairs % LANES, 0))
+    sent = jnp.concatenate(
+        [
+            unit_rows.astype(jnp.bfloat16).astype(jnp.float16),
+            other_rows.astype(jnp.bfloat16).astype(jnp.float16),
+            digits.astype(jnp.float16),
+        ],
+        axis=1,
+    )
+    every = lax.all_gather(sent, "dp", axis=0, tiled=True, axis_index_groups=[order])
+    own_all = every[:, :width].astype(jnp.bfloat16)
+    other_all = every[:, width : 2 * width].astype(jnp.bfloat16)
+    digits_all = every[:, 2 * width : 2 * width + 2].astype(jnp.int32)
+    pairs_all = digits_all[:, 0] * LANES + digits_all[:, 1]
+    sample_of = jnp.asarray(
+        np.concatenate([np.arange(row_count) + i * row_count for i in order]), jnp.int32
+    )
+    place = jnp.asarray(np.argsort(order), jnp.int32)[lax.axis_index("dp")] * row_count
+    scores_all = similarity(own_all, other_all, scale_value)
+    row_lse = log_sum_exp(scores_all, 1)
+    col_lse = log_sum_exp(scores_all, 0)
+    hit = sample_of[None, :] == pairs_all[:, None]
+    diagonal = jnp.sum(jnp.where(hit, scores_all, 0.0))
+    loss_value = (jnp.sum(row_lse) + jnp.sum(col_lse) - 2.0 * diagonal) / (2.0 * batch_total)
+    scores = lax.dynamic_slice_in_dim(scores_all, place, row_count)
+    own_lse = lax.dynamic_slice_in_dim(row_lse, place, row_count)
+    matched = sample_of[None, :] == pairs
+    pair_weight = (
+        jnp.exp(scores - own_lse[:, None])
+        + jnp.exp(scores - col_lse[None, :])
+        - 2.0 * matched.astype(jnp.float32)
+    ).astype(jnp.bfloat16)
+    unit_grad = (
+        scale_value
+        / (2.0 * batch_total)
+        * jnp.dot(pair_weight, other_all, preferred_element_type=jnp.float32)
+    )
+    embed_grad = (
+        unit_grad - unit_rows * jnp.sum(unit_rows * unit_grad, axis=-1, keepdims=True)
+    ) / lengths
+    return (loss_value, embed_grad[None])
+
+
+def gather_one(
     image_pooled, text_pooled, image_gain, text_gain, image_proj, text_proj, logit_scale, pair_index
 ):
     module_index = lax.axis_index("mod")
@@ -44,8 +131,7 @@
     batch_total = row_count * lax.axis_size("dp")
     gathered = lax.all_gather(mirror_rows, "dp", axis=0, tiled=True)
     scores = similarity(unit_half, gathered, scale_value)
-    running_max = jnp.max(scores, axis=1)
-    own_lse = running_max + jnp.log(jnp.sum(jnp.exp(scores - running_max[:, None]), axis=1))
+    own_lse = log_sum_exp(scores, 1)
     columns = lax.broadcasted_iota(jnp.int32, (row_count, batch_total), 1)
     matched = columns == pair_index[0][:, None]
     diagonal = jnp.sum(jnp.where(matched, scores, 0.0), axis=1)
@@ -74,4 +160,12 @@
 def solution(mesh):
     in_specs = (P("dp", None), P("dp", None), P(), P(), P(), P(), P(), P("mod", "dp"))
     out_specs = (P(), P("mod", "dp", None))
+    order = closed_path(mesh)
+
+    def local(*args):
+        batch_total = args[0].shape[0] * lax.axis_size("dp")
+        if 4 * batch_total * batch_total <= SCORE_BYTES:
+            return gather_both(order, *args)
+        return gather_one(*args)
+
     return jax.shard_map(local, mesh=mesh, in_specs=in_specs, out_specs=out_specs, check_vma=False)

time: 79 us -> 43.4 us (0.55)
  blocking collectives: 62.3 us -> 23.3 us
  other arithmetic: 4.46 us -> 8.05 us
  starting transfers between devices: 2.74 us -> 0 us
  matrix products: 2.94 us -> 5 us
  waiting for transfers between devices: 1.55 us -> 0 us
  between operations: 3.76 us -> 5.28 us
  local copies, waits for them, and re-layouts: 0.37 us -> 1.36 us
    unnamed x1 -> x0, blocking collectives: 37 us -> none
    ppermute x1 -> x0, starting transfers between devices: 2.74 us -> none  [from_partner(): lax.ppermute(x, axis, [(i, i ^ 1 << bit) for i in range(lax.axis_size(axi...]
    all_gather x1, blocking collectives: 25.3 us -> 23.3 us  [gather_both(): lax.all_gather(sent, 'dp', axis=0, tiled=True, axis_index_groups=[order])]
    ppermute x1 -> x0, waiting for transfers between devices: 1.55 us -> none  [from_partner(): lax.ppermute(x, axis, [(i, i ^ 1 << bit) for i in range(lax.axis_size(axi...]
    dynamic_slice x1 -> x2, local copies, waits for them, and re-layouts: 0.08 us -> 1.32 us  [the longest x1 1.24 us: gather_both(): jnp.asarray(np.argsort(order), jnp.int32)[lax.axis_index('dp')] * row_count]
    dot_general x1, matrix products: 0.42 us -> 1.62 us  [gather_both(): jnp.dot(pair_weight, other_all, preferred_element_type=jnp.float32)]
    reduce_sum x1 -> x2, other arithmetic: 1.08 us -> 2.11 us  [normalize_project(): variance = jnp.mean(centered * centered, axis=-1, keepdims=True)]
    reduce_sum x1 -> x2, other arithmetic: 1 us -> 1.96 us  [normalize_project(): centered = features - jnp.mean(features, axis=-1, keepdims=True)]
  transfers between devices with their start and end apart: 1 -> 0, of which waited for: 1 -> 0; matrix products, arithmetic and copies ran while one was open for 0% -> 0% of each run, Pallas kernels for 0% -> 0%
where the time goes in v1:
time: 43.4 us; the launch traced here: 43 us
  blocking collectives  23.3 us (54%)
  other arithmetic  8.05 us (19%)
  between operations  5.28 us (12%)
  matrix products  5 us (12%)
  local copies, waits for them, and re-layouts  1.36 us (3%)
    all_gather x1, blocking collectives, gather_both(): lax.all_gather(sent, 'dp', axis=0, tiled=True, axis_index_groups=[order])  23.3 us
    dot_general x2, matrix products, normalize_project(): return jnp.dot(normalized, weight, preferred_element_type=jnp.float32)  2.32 us
    reduce_sum x2, other arithmetic, normalize_project(): variance = jnp.mean(centered * centered, axis=-1, keepdims=True)  2.11 us
    reduce_sum x2, other arithmetic, normalize_project(): centered = features - jnp.mean(features, axis=-1, keepdims=True)  1.96 us
    dot_general x1, matrix products, gather_both(): jnp.dot(pair_weight, other_all, preferred_element_type=jnp.float32)  1.62 us
    reduce_sum x1, other arithmetic, gather_both(): diagonal = jnp.sum(jnp.where(hit, scores_all, 0.0))  1.36 us
    dynamic_slice x1, local copies, waits for them, and re-layouts, gather_both(): jnp.asarray(np.argsort(order), jnp.int32)[lax.axis_index('dp')] * row_count  1.24 us
    dot_general x1, matrix products, similarity(): lax.dot_general(left_rows, right_rows, (((1,), (1,)), ((), ())), preferre...  1.06 us

profile of v1, /device:TPU:0, one launch (start us, length us, event | category | flops | bytes accessed | tf_op | source)
XLA Modules:
  0.0 43.0 jit_solution(16931766107789122191)
XLA Ops:
  0.6 0.0 copy-start
  0.6 0.0 copy-start.2
  0.7 0.0 copy-start.3
  1.4 1.2 %dynamic_slice.9 = s32[1]{0:T(128)} dynamic-slice(s32[16]{0:T(128)} %constant.77.clone, s32[]{:T(128)S(6)} %select_n.74), dynamic_slice_sizes={1} | dynamic-slice | bytes 12 | tf_op jit(solution)/shard_map/dynamic_slice | solution.py:91
  3.3 1.0 %convert_reduce_fusion = f32[40]{0:T(128)S(1)} fusion(bf16[40,1024]{1,0:T(8,128)(2,1)} %param.10), kind=kLoop, calls=%fused_computation.11 | loop fusion | flops 81880 | bytes 82080 | tf_op jit(solution)/shard_map/reduce_sum | solution.py:38
  4.4 1.1 %fusion.3 = f32[40]{0:T(128)S(1)} fusion(bf16[40,1024]{1,0:T(8,128)(2,1)} %param.10, f32[40]{0:T(128)S(1)} %broadcast_multiply_fusion.1), kind=kLoop, calls=%fused_computation.14 | loop fusion | flops 163800 | bytes 82240 | tf_op jit(solution)/shard_map/reduce_sum | solution.py:39
  5.5 1.0 %convert_reduce_fusion.1 = f32[40]{0:T(128)S(1)} fusion(bf16[40,768]{1,0:T(8,128)(2,1)} %param.11), kind=kLoop, calls=%fused_computation.19 | loop fusion | flops 61400 | bytes 61600 | tf_op jit(solution)/shard_map/reduce_sum | solution.py:38
  6.4 1.0 %fusion.8 = f32[40]{0:T(128)S(1)} fusion(bf16[40,768]{1,0:T(8,128)(2,1)} %param.11, f32[40]{0:T(128)S(1)} %broadcast_multiply_fusion), kind=kLoop, calls=%fused_computation.23 | loop fusion | flops 122840 | bytes 61760 | tf_op jit(solution)/shard_map/reduce_sum | solution.py:39
  7.5 0.7 %and_select_fusion.1 = (s32[40]{0:T(128)S(1)}, s32[40]{0:T(128)S(1)}) fusion(s32[1,40]{1,0:T(1,128)} %param.17), kind=kLoop, calls=%fused_computation.55 | loop fusion | flops 760 | bytes 480 | tf_op jit(solution)/shard_map/jit(floor_divide)/jit(_where)/select_n | solution.py:74
  8.1 0.1 select_convert_fusion.1
  8.2 1.8 %multiply_reduce_fusion.1 = (f32[40]{0:T(128)S(1)}, f32[40,768]{1,0:T(8,128)S(1)}) fusion(bf16[768,768]{1,0:T(8,128)(2,1)} %param.15, bf16[40,768]{1,0:T(8,128)(2,1)} %param.11, f32[768]{0:T(1024)} %param.13, f32[40]{0:T(128)S(1)} %add_rsqrt_fusion, f32[40]{0:T(128)S(1)} %broadcast_multiply_fusion), kind=kOutput, calls=%fused_computation.29 | convolution fusion | flops 47400920 | bytes 1367520 | tf_op jit(solution)/shard_map/dot_general | solution.py:41
  10.0 0.0 copy-done
  10.1 0.5 %multiply_reduce_fusion.2 = (f32[40]{0:T(128)S(1)}, f32[40,768]{1,0:T(8,128)S(1)}) fusion(bf16[1024,768]{1,0:T(8,128)(2,1)S(1)} %copy-done, bf16[40,1024]{1,0:T(8,128)(2,1)S(1)} %copy-done.2, f32[1024]{0:T(1024)S(1)} %copy-done.3, f32[40]{0:T(128)S(1)} %add_rsqrt_fusion.1, f32[40]{0:T(128)S(1)} %broadcast_multiply_fusion.1), kind=kOutput, calls=%fused_computation.30 | convolution fusion | flops 63180760 | bytes 1782240 | tf_op jit(solution)/shard_map/dot_general | solution.py:41
  10.6 0.1 convert_convert_fusion
  10.8 23.3 %all-gather.1 = f16[640,1664]{1,0:T(8,128)(2,1)S(1)} all-gather(f16[40,1664]{1,0:T(8,128)(2,1)S(1)} %pad_maximum_fusion), channel_id=1, replica_groups={{0,1,4,5,8,9,12,13,14,15,10,11,6,7,2,3},{16,17,20,21,24,25,28,29,30,31,..., dimensions={0}, use_global_device_ids=true | all-gather | bytes 2263040 | tf_op jit(solution)/shard_map/all_gather | solution.py:83
  34.1 0.3 fusion
  34.4 0.0 copy-start.4
  34.4 1.1 %fusion.31 = (f32[640]{0:T(1024)S(1)}, f32[640]{0:T(1024)S(1)}, f32[640,640]{1,0:T(8,128)S(1)}) fusion(f16[640,1664]{1,0:T(8,128)(2,1)S(1)} %all-gather.1, f32[]{:T(128)} %bitcast.13), kind=kOutput, calls=%fused_computation.71 | convolution fusion | flops 631356160 | bytes 3609604 | tf_op jit(solution)/shard_map/dot_general | solution.py:50
  35.4 0.0 copy-start.5
  35.5 1.4 %select_reduce_fusion = (f32[]{:T(128)}, f32[640]{0:T(1024)S(1)}, f32[640]{0:T(1024)S(1)}) fusion(f32[640,640]{1,0:T(8,128)S(1)} %get-tuple-element.23, s32[640]{0:T(1024)S(1)} %copy-done.4, s32[640]{0:T(1024)S(1)} %fusion, f32[640]{0:T(1024)S(1)} %get-tuple-element.5, f32[640]{0:T(1024)S(1)} %get-tuple-element.6), kind=kLoop, calls=%fused_computation | loop fusion | flops 2865919 | bytes 1653764 | tf_op jit(solution)/shard_map/reduce_sum | solution.py:96
  37.5 0.6 %fusion.32 = (f32[]{:T(128)}, f32[640]{0:T(1024)S(1)}, f32[]{:T(128)}, f32[640]{0:T(1024)S(1)}) fusion(f32[640]{0:T(1024)S(1)} %get-tuple-element.5, f32[640]{0:T(1024)S(1)} %get-tuple-element.3, f32[640]{0:T(1024)S(1)} %get-tuple-element.6, f32[640]{0:T(1024)S(1)} %get-tuple-element.4), kind=kLoop, calls=%fused_computation.72 | loop fusion | flops 2558 | bytes 15368 | tf_op jit(solution)/shard_map/reduce_sum | solution.py:97
  39.4 0.1 dynamic_slice.11
  39.5 1.6 %multiply_reduce_fusion = (f32[40]{0:T(128)S(1)}, f32[40,768]{1,0:T(8,128)S(1)}) fusion(f32[40,768]{1,0:T(8,128)S(1)} %get-tuple-element.12, f16[640,1664]{1,0:T(8,128)(2,1)} %copy-done.1, f32[640,640]{1,0:T(8,128)S(1)} %get-tuple-element.23, s32[]{:T(128)S(6)} %select_n.75, s32[640]{0:T(1024)S(1)} %copy-done.4, f32[640]{0:T(1024)S(1)} %get-tuple-element.8, ...), kind=kOutput, calls=%fused_computation.27 | convolution fusion | flops 40084440 | bytes 1340584 | tf_op jit(solution)/shard_map/dot_general | solution.py:109
  41.1 0.8 %divide_bitcast_fusion = f32[1,40,768]{2,1,0:T(8,128)} fusion(f32[40,768]{1,0:T(8,128)S(1)} %get-tuple-element.25, f32[40,768]{1,0:T(8,128)S(1)} %get-tuple-element.12, f32[40]{0:T(128)S(1)} %get-tuple-element.14, f32[40]{0:T(128)S(1)} %get-tuple-element.24), kind=kLoop, calls=%fused_computation.26 | loop fusion | flops 92160 | bytes 368960 | tf_op jit(solution)/shard_map/broadcast_in_dim | solution.py:114
  (15 shorter events, 0.1 us)
Async XLA Ops:
  0.6 9.4 %copy-start = (bf16[1024,768]{1,0:T(8,128)(2,1)S(1)}, bf16[1024,768]{1,0:T(8,128)(2,1)}, u32[]{:S(2)}) copy-start(bf16[1024,768]{1,0:T(8,128)(2,1)} %param.14) | copy-start | bytes 4718596
  0.6 9.4 %copy-start.2 = (bf16[40,1024]{1,0:T(8,128)(2,1)S(1)}, bf16[40,1024]{1,0:T(8,128)(2,1)}, u32[]{:S(2)}) copy-start(bf16[40,1024]{1,0:T(8,128)(2,1)} %param.10) | copy-start | bytes 245764
  0.7 9.4 %copy-start.3 = (f32[1024]{0:T(1024)S(1)}, f32[1024]{0:T(1024)}, u32[]{:S(2)}) copy-start(f32[1024]{0:T(1024)} %param.12) | copy-start | bytes 12292
  34.0 1.4 %copy-start.1 = (f16[640,1664]{1,0:T(8,128)(2,1)}, f16[640,1664]{1,0:T(8,128)(2,1)S(1)}, u32[]{:S(2)}) copy-start(f16[640,1664]{1,0:T(8,128)(2,1)S(1)} %all-gather.1) | copy-start | bytes 6389764
  34.4 1.1 %copy-start.4 = (s32[640]{0:T(1024)S(1)}, s32[640]{0:T(1024)}, u32[]{:S(2)}) copy-start(s32[640]{0:T(1024)} %constant.76.clone) | copy-start | bytes 7684
  35.4 4.0 %copy-start.5 = (s32[1,40]{1,0:T(1,128)S(1)}, s32[1,40]{1,0:T(1,128)}, u32[]{:S(2)}) copy-start(s32[1,40]{1,0:T(1,128)} %param.17) | copy-start | bytes 484

commit v2 on v0

--- a/solution.py
+++ b/solution.py
@@ -1,7 +1,37 @@
 import jax
 import jax.numpy as jnp
+import numpy as np
 from jax import lax
+from jax.experimental import pallas as pl
+from jax.experimental.pallas import tpu as pltpu
 from jax.sharding import PartitionSpec as P
+
+LANES = 128
+SIDE_INVERSE, SIDE_PLACE, SIDE_SCALE = 0, 1, 2
+LOG2_E = float(np.log2(np.e))
+SCORE_BYTES = 2**22
+KERNEL_BYTES = 2**24
+
+
+def closed_path(mesh):
+    places = [getattr(d, "coords", None) for d in mesh.devices[0]]
+    natural = list(range(len(places)))
+    if any(p is None for p in places):
+        return natural
+    chips = {}
+    for i, p in enumerate(places):
+        chips.setdefault(tuple(p), []).append(i)
+    span = [sorted({c[k] for c in chips}) for k in range(3)]
+    wide = [k for k in range(3) if len(span[k]) > 1]
+    if len(wide) != 2 or len(chips) != len(span[wide[0]]) * len(span[wide[1]]):
+        return natural
+    short, long = sorted(wide, key=lambda k: len(span[k]))
+    if len(span[short]) != 2:
+        return natural
+    by = {(c[short], c[long]): v for c, v in chips.items()}
+    there = [by[span[short][0], z] for z in span[long]]
+    back = [by[span[short][1], z] for z in reversed(span[long])]
+    return [i for cores in there + back for i in cores]
 
 
 def from_partner(x, axis, bit):
@@ -27,7 +57,224 @@
     )
 
 
-def local(
+def log_sum_exp(scores, axis):
+    top = jnp.max(scores, axis=axis)
+    return top + jnp.log(jnp.sum(jnp.exp(scores - jnp.expand_dims(top, axis)), axis=axis))
+
+
+def normalize(pooled, gain):
+    features = pooled.astype(jnp.float32)
+    centered = features - jnp.mean(features, axis=-1, keepdims=True)
+    variance = jnp.mean(centered * centered, axis=-1, keepdims=True)
+    return (centered * lax.rsqrt(variance + 1e-05) * gain).astype(jnp.bfloat16)
+
+
+def lane_table(entries, shape):
+    lane = lax.broadcasted_iota(jnp.int32, shape, 1)
+    table = jnp.zeros(shape, jnp.float32)
+    for i, entry in entries.items():
+        table = jnp.where(lane == i, entry, table)
+    return table
+
+
+def embed_kernel(
+    order,
+    image_pooled,
+    text_pooled,
+    image_gain,
+    text_gain,
+    image_proj,
+    text_proj,
+    logit_scale,
+    pair_index,
+    sent,
+    unit,
+    side,
+    image_rows,
+    text_rows,
+    image_scale,
+    text_scale,
+    image_weight,
+    text_weight,
+    scale_word,
+    pair_row,
+    arrived,
+):
+    row_count, width = unit.shape
+    moves = [
+        (pair_index, pair_row),
+        (logit_scale, scale_word),
+        (image_pooled, image_rows),
+        (image_gain, image_scale),
+        (text_pooled, text_rows),
+        (text_gain, text_scale),
+    ]
+    copies = [pltpu.make_async_copy(a, b, arrived.at[i]) for i, (a, b) in enumerate(moves)]
+    slabs = []
+    for source, target in ((image_proj, image_weight), (text_proj, text_weight)):
+        depth = 256 if source.shape[0] % 256 == 0 else source.shape[0]
+        for start in range(0, source.shape[0], depth):
+            rows = pl.ds(start, depth)
+            copy = pltpu.make_async_copy(
+                source.at[rows], target.at[rows], arrived.at[len(moves) + len(slabs)]
+            )
+            slabs.append((target, start, depth, copy))
+    for copy in copies + [slab[3] for slab in slabs]:
+        copy.start()
+
+    copies[0].wait()
+    copies[1].wait()
+    pairs = pair_row[...]
+    places = pairs
+    for here, sample in enumerate(order):
+        inside = (pairs >= sample * row_count) & (pairs < (sample + 1) * row_count)
+        places = jnp.where(inside, pairs + (here - sample) * row_count, places)
+    square = (row_count, row_count)
+    upright = lax.broadcasted_iota(jnp.int32, square, 0) == lax.broadcasted_iota(jnp.int32, square, 1)
+    place = jnp.sum(jnp.where(upright, places.astype(jnp.float32), 0.0), axis=1, keepdims=True)
+    high = jnp.floor(place * (1.0 / LANES))
+    digits = lane_table({0: high, 1: place - high * LANES}, (row_count, LANES))
+    sent[:, 2 * width :] = digits.astype(jnp.bfloat16)
+
+    copies[2].wait()
+    copies[3].wait()
+    image_normed = normalize(image_rows[...], image_scale[...][None, :])
+    copies[4].wait()
+    copies[5].wait()
+    text_normed = normalize(text_rows[...], text_scale[...][None, :])
+
+    def project(normed, weight):
+        total = None
+        for target, start, depth, copy in slabs:
+            if target is weight:
+                copy.wait()
+                part = jnp.dot(
+                    normed[:, start : start + depth],
+                    target[start : start + depth, :],
+                    preferred_element_type=jnp.float32,
+                )
+                total = part if total is None else total + part
+        return total
+
+    def unitize_rows(embedded):
+        squares = jnp.sum(embedded * embedded, axis=-1, keepdims=True) + 1e-06
+        inverse = 1.0 / jnp.sqrt(squares)
+        return embedded * inverse, inverse
+
+    is_image = lax.axis_index("mod") == 0
+    image_unit, image_inverse = unitize_rows(project(image_normed, image_weight))
+    text_unit, text_inverse = unitize_rows(project(text_normed, text_weight))
+    own = jnp.where(is_image, image_unit, text_unit)
+    unit[...] = own
+    sent[:, :width] = own.astype(jnp.bfloat16)
+    sent[:, width : 2 * width] = jnp.where(is_image, text_unit, image_unit).astype(jnp.bfloat16)
+    side[...] = lane_table(
+        {
+            SIDE_INVERSE: jnp.where(is_image, image_inverse, text_inverse),
+            SIDE_PLACE: place,
+            SIDE_SCALE: scale_word[...][None, :],
+        },
+        (row_count, LANES),
+    )
+
+
+def score_kernel(order, every, unit, side, loss_value, embed_grad, scores):
+    row_count, width = unit.shape
+    batch_total = every.shape[0]
+    chunk = LANES
+    scale_value = side[0:1, SIDE_SCALE : SIDE_SCALE + 1]
+    factor = scale_value * LOG2_E
+    column = lax.broadcasted_iota(jnp.int32, (1, batch_total), 1).astype(jnp.float32)
+
+    top = jnp.full((1, batch_total), -jnp.inf, jnp.float32)
+    diagonal = jnp.zeros((1, batch_total), jnp.float32)
+    rows_total = jnp.zeros((chunk, 1), jnp.float32)
+    for start in range(0, batch_total, chunk):
+        block = factor * lax.dot_general(
+            every[start : start + chunk, :width],
+            every[:, width : 2 * width],
+            (((1,), (1,)), ((), ())),
+            preferred_element_type=jnp.float32,
+        )
+        scores[start : start + chunk, :] = block
+        top = jnp.maximum(top, jnp.max(block, axis=0, keepdims=True))
+        digits = every[start : start + chunk, 2 * width :].astype(jnp.float32)
+        places = digits[:, 0:1] * LANES + digits[:, 1:2]
+        diagonal = diagonal + jnp.sum(jnp.where(column == places, block, 0.0), axis=0, keepdims=True)
+        row_top = jnp.max(block, axis=1, keepdims=True)
+        row_sum = jnp.sum(jnp.exp2(block - row_top), axis=1, keepdims=True)
+        rows_total = rows_total + (row_top + LOG2_E * jnp.log(row_sum))
+    column_sum = jnp.zeros((1, batch_total), jnp.float32)
+    for start in range(0, batch_total, chunk):
+        block = scores[start : start + chunk, :]
+        column_sum = column_sum + jnp.sum(jnp.exp2(block - top), axis=0, keepdims=True)
+    column_lse = top + LOG2_E * jnp.log(column_sum)
+    total = jnp.sum(rows_total) + jnp.sum(column_lse - 2.0 * diagonal)
+    loss_value[0] = total * (float(np.log(2.0)) / (2.0 * batch_total))
+
+    mine = lax.axis_index("dp")
+    first = jnp.int32(0)
+    for here, sample in enumerate(order):
+        first = jnp.where(mine == sample, here * row_count, first)
+    block = scores[pl.ds(pl.multiple_of(first, 8), row_count), :]
+    row_top = jnp.max(block, axis=1, keepdims=True)
+    row_sum = jnp.sum(jnp.exp2(block - row_top), axis=1, keepdims=True)
+    row_lse = row_top + LOG2_E * jnp.log(row_sum)
+    matched = jnp.where(column == side[:, SIDE_PLACE : SIDE_PLACE + 1], 2.0, 0.0)
+    pair_weight = jnp.exp2(block - row_lse) + jnp.exp2(block - column_lse) - matched
+    unit_grad = (scale_value * (0.5 / batch_total)) * jnp.dot(
+        pair_weight.astype(jnp.bfloat16),
+        every[:, width : 2 * width],
+        preferred_element_type=jnp.float32,
+    )
+    unit_rows = unit[...]
+    along = jnp.sum(unit_rows * unit_grad, axis=-1, keepdims=True)
+    embed_grad[0] = (unit_grad - unit_rows * along) * side[:, SIDE_INVERSE : SIDE_INVERSE + 1]
+
+
+def gather_both(
+    order, image_pooled, text_pooled, image_gain, text_gain, image_proj, text_proj, logit_scale, pair_index
+):
+    row_count = image_pooled.shape[0]
+    width = image_proj.shape[1]
+    batch_total = row_count * len(order)
+    f32, bf16 = jnp.float32, jnp.bfloat16
+    operands = (
+        image_pooled, text_pooled, image_gain, text_gain, image_proj, text_proj, logit_scale, pair_index
+    )
+    sent, unit, side = pl.pallas_call(
+        lambda *refs: embed_kernel(order, *refs),
+        out_shape=(
+            jax.ShapeDtypeStruct((row_count, 2 * width + LANES), bf16),
+            jax.ShapeDtypeStruct((row_count, width), f32),
+            jax.ShapeDtypeStruct((row_count, LANES), f32),
+        ),
+        in_specs=[pl.BlockSpec(memory_space=pltpu.HBM)] * len(operands),
+        out_specs=[pl.BlockSpec(memory_space=pltpu.VMEM)] * 3,
+        scratch_shapes=[pltpu.VMEM(x.shape, x.dtype) for x in operands]
+        + [pltpu.SemaphoreType.DMA((64,))],
+        compiler_params=pltpu.CompilerParams(vmem_limit_bytes=KERNEL_BYTES),
+        name="embed",
+    )(*(x if x.shape == (1,) else pltpu.with_memory_space_constraint(x, pltpu.HBM) for x in operands))
+    every = lax.all_gather(
+        sent.astype(jnp.float16), "dp", axis=0, tiled=True, axis_index_groups=[order]
+    ).astype(bf16)
+    loss_value, embed_grad = pl.pallas_call(
+        lambda *refs: score_kernel(order, *refs),
+        out_shape=(
+            jax.ShapeDtypeStruct((1,), f32),
+            jax.ShapeDtypeStruct((1, row_count, width), f32),
+        ),
+        in_specs=[pl.BlockSpec(memory_space=pltpu.VMEM)] * 3,
+        out_specs=[pl.BlockSpec(memory_space=pltpu.SMEM), pl.BlockSpec(memory_space=pltpu.VMEM)],
+        scratch_shapes=[pltpu.VMEM((batch_total, batch_total), f32)],
+        compiler_params=pltpu.CompilerParams(vmem_limit_bytes=KERNEL_BYTES),
+        name="scores",
+    )(every, unit, side)
+    return (loss_value[0], embed_grad)
+
+
+def gather_one(
     image_pooled, text_pooled, image_gain, text_gain, image_proj, text_proj, logit_scale, pair_index
 ):
     module_index = lax.axis_index("mod")
@@ -44,8 +291,7 @@
     batch_total = row_count * lax.axis_size("dp")
     gathered = lax.all_gather(mirror_rows, "dp", axis=0, tiled=True)
     scores = similarity(unit_half, gathered, scale_value)
-    running_max = jnp.max(scores, axis=1)
-    own_lse = running_max + jnp.log(jnp.sum(jnp.exp(scores - running_max[:, None]), axis=1))
+    own_lse = log_sum_exp(scores, 1)
     columns = lax.broadcasted_iota(jnp.int32, (row_count, batch_total), 1)
     matched = columns == pair_index[0][:, None]
     diagonal = jnp.sum(jnp.where(matched, scores, 0.0), axis=1)
@@ -74,4 +320,13 @@
 def solution(mesh):
     in_specs = (P("dp", None), P("dp", None), P(), P(), P(), P(), P(), P("mod", "dp"))
     out_specs = (P(), P("mod", "dp", None))
+    order = closed_path(mesh)
+
+    def local(*args):
+        batch_total = args[0].shape[0] * lax.axis_size("dp")
+        small = 4 * batch_total * batch_total <= SCORE_BYTES
+        if small and batch_total % LANES == 0 and args[0].shape[0] % 8 == 0:
+            return gather_both(order, *args)
+        return gather_one(*args)
+
     return jax.shard_map(local, mesh=mesh, in_specs=in_specs, out_specs=out_specs, check_vma=False)

time: 79 us -> 31.5 us (0.40)
  blocking collectives: 62.3 us -> 23.3 us
  Pallas kernels: 0 us -> 6.48 us
  other arithmetic: 4.46 us -> 0.31 us
  matrix products: 2.94 us -> 0 us
  starting transfers between devices: 2.74 us -> 0 us
  between operations: 3.76 us -> 1.3 us
  waiting for transfers between devices: 1.55 us -> 0 us
    unnamed x1 -> x0, blocking collectives: 37 us -> none
    pallas_call x0 -> x2, Pallas kernels: none -> 6.48 us  [the longest x1 3.24 us: gather_both(): pl.pallas_call(lambda *refs: score_kernel(order, *refs), out_shape=(jax.S...]
    reduce_sum x5 -> x0, other arithmetic: 3.49 us -> none  [the longest x1 1.08 us: normalize_project(): variance = jnp.mean(centered * centered, axis=-1, keepdims=True)]
    dot_general x3 -> x0, matrix products: 2.94 us -> none  [the longest x1 2 us: normalize_project(): return jnp.dot(normalized, weight, preferred_element_type=jnp.float32)]
    ppermute x1 -> x0, starting transfers between devices: 2.74 us -> none  [from_partner(): lax.ppermute(x, axis, [(i, i ^ 1 << bit) for i in range(lax.axis_size(axi...]
    all_gather x1, blocking collectives: 25.3 us -> 23.3 us  [gather_both(): lax.all_gather(sent.astype(jnp.float16), 'dp', axis=0, tiled=True, axis_i...]
    ppermute x1 -> x0, waiting for transfers between devices: 1.55 us -> none  [from_partner(): lax.ppermute(x, axis, [(i, i ^ 1 << bit) for i in range(lax.axis_size(axi...]
  transfers between devices with their start and end apart: 1 -> 0, of which waited for: 1 -> 0; matrix products, arithmetic and copies ran while one was open for 0% -> 0% of each run, Pallas kernels for 0% -> 0%
where the time goes in v2:
time: 31.5 us; the launch traced here: 31.4 us
  blocking collectives  23.3 us (74%)
  Pallas kernels  6.48 us (21%)
  between operations  1.3 us (4%)
    all_gather x1, blocking collectives, gather_both(): lax.all_gather(sent.astype(jnp.float16), 'dp', axis=0, tiled=True, axis_i...  23.3 us
    pallas_call x1, Pallas kernels, gather_both(): pl.pallas_call(lambda *refs: score_kernel(order, *refs), out_shape=(jax.S...  3.24 us
    pallas_call x1, Pallas kernels, gather_both(): pl.pallas_call(lambda *refs: embed_kernel(order, *refs), out_shape=(jax.S...  3.23 us

profile of v2, /device:TPU:0, one launch (start us, length us, event | category | flops | bytes accessed | tf_op | source)
XLA Modules:
  0.0 31.4 jit_solution(3413781415604470870)
XLA Ops:
  1.3 3.2 %embed.1 = (bf16[40,1664]{1,0:T(8,128)(2,1)S(1)}, f32[40,768]{1,0:T(8,128)S(1)}, f32[40,128]{1,0:T(8,128)S(1)}) custom-call(bf16[40,1024]{1,0:T(8,128)(2,1)} %refs_0_.1, bf16[40,768]{1,0:T(8,128)(2,1)} %refs_1_.1, f32[1024]{0:T(1024)} %refs_2_.1, f32[768]{0:T(1024)} %refs_3_.1, bf16[1024,768]{1,0:T(8,128)(2,1)} %refs_4_.1, bf16[768,768]{1,0:T(8,128)(2,1)} %refs_5_.1, ...), custom_call_target="tpu_custom_call" | custom-call | tf_op jit(solution)/shard_map/embed/pallas_call | solution.py:245
  4.6 23.3 %all-gather.1 = f16[640,1664]{1,0:T(8,128)(2,1)S(1)} all-gather(f16[40,1664]{1,0:T(8,128)(2,1)S(1)} %convert_element_type.6), channel_id=1, replica_groups={{0,1,4,5,8,9,12,13,14,15,10,11,6,7,2,3},{16,17,20,21,24,25,28,29,30,31,..., dimensions={0}, use_global_device_ids=true | all-gather | bytes 2263040 | tf_op jit(solution)/shard_map/all_gather | solution.py:259
  27.8 0.3 convert_element_type.7.refs_0_
  28.1 3.2 %scores.1 = (f32[1]{0:T(128)}, f32[1,40,768]{2,1,0:T(8,128)}) custom-call(bf16[640,1664]{1,0:T(8,128)(2,1)S(1)} %convert_element_type.7.refs_0_, f32[40,768]{1,0:T(8,128)S(1)} %get-tuple-element.8.refs_1_, f32[40,128]{1,0:T(8,128)S(1)} %get-tuple-element.9.refs_2_), custom_call_target="tpu_custom_call" | custom-call | tf_op jit(solution)/shard_map/scores/pallas_call | solution.py:262
  (1 shorter events, 0.0 us)

commit v3 on v2

--- a/solution.py
+++ b/solution.py
@@ -8,7 +8,9 @@
 
 LANES = 128
 SIDE_INVERSE, SIDE_PLACE, SIDE_SCALE = 0, 1, 2
+LOW_LANE = 64
 LOG2_E = float(np.log2(np.e))
+CHUNK = 256
 SCORE_BYTES = 2**22
 KERNEL_BYTES = 2**24
 
@@ -85,7 +87,6 @@
     text_gain,
     image_proj,
     text_proj,
-    logit_scale,
     pair_index,
     sent,
     unit,
@@ -96,34 +97,24 @@
     text_scale,
     image_weight,
     text_weight,
-    scale_word,
     pair_row,
     arrived,
 ):
     row_count, width = unit.shape
     moves = [
         (pair_index, pair_row),
-        (logit_scale, scale_word),
         (image_pooled, image_rows),
         (image_gain, image_scale),
         (text_pooled, text_rows),
         (text_gain, text_scale),
+        (image_proj, image_weight),
+        (text_proj, text_weight),
     ]
     copies = [pltpu.make_async_copy(a, b, arrived.at[i]) for i, (a, b) in enumerate(moves)]
-    slabs = []
-    for source, target in ((image_proj, image_weight), (text_proj, text_weight)):
-        depth = 256 if source.shape[0] % 256 == 0 else source.shape[0]
-        for start in range(0, source.shape[0], depth):
-            rows = pl.ds(start, depth)
-            copy = pltpu.make_async_copy(
-                source.at[rows], target.at[rows], arrived.at[len(moves) + len(slabs)]
-            )
-            slabs.append((target, start, depth, copy))
-    for copy in copies + [slab[3] for slab in slabs]:
+    for copy in copies:
         copy.start()
 
     copies[0].wait()
-    copies[1].wait()
     pairs = pair_row[...]
     places = pairs
     for here, sample in enumerate(order):
@@ -133,28 +124,23 @@
     upright = lax.broadcasted_iota(jnp.int32, square, 0) == lax.broadcasted_iota(jnp.int32, square, 1)
     place = jnp.sum(jnp.where(upright, places.astype(jnp.float32), 0.0), axis=1, keepdims=True)
     high = jnp.floor(place * (1.0 / LANES))
-    digits = lane_table({0: high, 1: place - high * LANES}, (row_count, LANES))
-    sent[:, 2 * width :] = digits.astype(jnp.bfloat16)
-
+    across, down = width // LANES, row_count // 8
+    for k in range(down):
+        rows = slice(k * 8, k * 8 + 8)
+        lane = lax.broadcasted_iota(jnp.int32, (8, LANES), 1)
+        tile = jnp.where(lane == k, high[rows], 0.0 if k == 0 else tile)
+        tile = jnp.where(lane == LOW_LANE + k, place[rows] - high[rows] * LANES, tile)
+    sent[2 * across * down] = tile.astype(jnp.bfloat16)
+
+    copies[1].wait()
     copies[2].wait()
+    image_normed = normalize(image_rows[...], image_scale[...][None, :])
     copies[3].wait()
-    image_normed = normalize(image_rows[...], image_scale[...][None, :])
     copies[4].wait()
-    copies[5].wait()
     text_normed = normalize(text_rows[...], text_scale[...][None, :])
 
     def project(normed, weight):
-        total = None
-        for target, start, depth, copy in slabs:
-            if target is weight:
-                copy.wait()
-                part = jnp.dot(
-                    normed[:, start : start + depth],
-                    target[start : start + depth, :],
-                    preferred_element_type=jnp.float32,
-                )
-                total = part if total is None else total + part
-        return total
+        return jnp.dot(normed, weight, preferred_element_type=jnp.float32)
 
     def unitize_rows(embedded):
         squares = jnp.sum(embedded * embedded, axis=-1, keepdims=True) + 1e-06
@@ -162,54 +148,67 @@
         return embedded * inverse, inverse
 
     is_image = lax.axis_index("mod") == 0
-    image_unit, image_inverse = unitize_rows(project(image_normed, image_weight))
-    text_unit, text_inverse = unitize_rows(project(text_normed, text_weight))
+    copies[5].wait()
+    image_unit, image_inverse = unitize_rows(project(image_normed, image_weight[...]))
+    copies[6].wait()
+    text_unit, text_inverse = unitize_rows(project(text_normed, text_weight[...]))
     own = jnp.where(is_image, image_unit, text_unit)
     unit[...] = own
-    sent[:, :width] = own.astype(jnp.bfloat16)
-    sent[:, width : 2 * width] = jnp.where(is_image, text_unit, image_unit).astype(jnp.bfloat16)
+    other = jnp.where(is_image, text_unit, image_unit)
+    for base, rows in ((0, own), (across * down, other)):
+        for i in range(down):
+            for k in range(across):
+                tile = rows[i * 8 : i * 8 + 8, k * LANES : (k + 1) * LANES]
+                sent[base + i * across + k] = tile.astype(jnp.bfloat16)
     side[...] = lane_table(
         {
             SIDE_INVERSE: jnp.where(is_image, image_inverse, text_inverse),
             SIDE_PLACE: place,
-            SIDE_SCALE: scale_word[...][None, :],
         },
         (row_count, LANES),
     )
 
 
-def score_kernel(order, every, unit, side, loss_value, embed_grad, scores):
+def score_kernel(order, logit_scale, own_all, other_all, digits, unit, side, loss_value, embed_grad, scores):
     row_count, width = unit.shape
-    batch_total = every.shape[0]
-    chunk = LANES
-    scale_value = side[0:1, SIDE_SCALE : SIDE_SCALE + 1]
+    batch_total = own_all.shape[0]
+    scale_value = logit_scale[0]
     factor = scale_value * LOG2_E
     column = lax.broadcasted_iota(jnp.int32, (1, batch_total), 1).astype(jnp.float32)
 
-    top = jnp.full((1, batch_total), -jnp.inf, jnp.float32)
-    diagonal = jnp.zeros((1, batch_total), jnp.float32)
-    rows_total = jnp.zeros((chunk, 1), jnp.float32)
-    for start in range(0, batch_total, chunk):
+    columns = digits[...].astype(jnp.float32)
+    columns = columns * LANES + pltpu.roll(columns, LANES - LOW_LANE, axis=2)
+    places = jnp.concatenate(
+        [columns[i, :, k : k + 1] for i in range(len(order)) for k in range(row_count // 8)], axis=0
+    )
+    lanes = lax.broadcasted_iota(jnp.int32, (1, LANES), 1).astype(jnp.float32)
+    row_tops = jnp.full((batch_total, LANES), -jnp.inf, jnp.float32)
+    diagonal = jnp.zeros((8, LANES), jnp.float32)
+    column_lses = []
+    for start in range(0, batch_total, CHUNK):
+        count = min(CHUNK, batch_total - start)
         block = factor * lax.dot_general(
-            every[start : start + chunk, :width],
-            every[:, width : 2 * width],
+            own_all[...],
+            other_all[start : start + count, :],
             (((1,), (1,)), ((), ())),
             preferred_element_type=jnp.float32,
         )
-        scores[start : start + chunk, :] = block
-        top = jnp.maximum(top, jnp.max(block, axis=0, keepdims=True))
-        digits = every[start : start + chunk, 2 * width :].astype(jnp.float32)
-        places = digits[:, 0:1] * LANES + digits[:, 1:2]
-        diagonal = diagonal + jnp.sum(jnp.where(column == places, block, 0.0), axis=0, keepdims=True)
-        row_top = jnp.max(block, axis=1, keepdims=True)
-        row_sum = jnp.sum(jnp.exp2(block - row_top), axis=1, keepdims=True)
-        rows_total = rows_total + (row_top + LOG2_E * jnp.log(row_sum))
-    column_sum = jnp.zeros((1, batch_total), jnp.float32)
-    for start in range(0, batch_total, chunk):
-        block = scores[start : start + chunk, :]
-        column_sum = column_sum + jnp.sum(jnp.exp2(block - top), axis=0, keepdims=True)
-    column_lse = top + LOG2_E * jnp.log(column_sum)
-    total = jnp.sum(rows_total) + jnp.sum(column_lse - 2.0 * diagonal)
+        scores[:, start : start + count] = block
+        top = jnp.max(block, axis=0, keepdims=True)
+        total = jnp.sum(jnp.exp2(block - top), axis=0, keepdims=True)
+        column_lses.append(top + LOG2_E * jnp.log(total))
+        for k in range(0, count, LANES):
+            part = block[:, k : k + LANES]
+            row_tops = jnp.maximum(row_tops, part)
+            hit = jnp.where(places == lanes + (start + k), part, 0.0)
+            diagonal = diagonal + jnp.sum(hit.reshape(batch_total // 8, 8, LANES), axis=0)
+    column_lse = jnp.concatenate(column_lses, axis=1)
+    row_top = jnp.max(row_tops, axis=1, keepdims=True)
+    sums = jnp.zeros((batch_total, LANES), jnp.float32)
+    for start in range(0, batch_total, LANES):
+        sums = sums + jnp.exp2(scores[:, start : start + LANES] - row_top)
+    row_lse = row_top + LOG2_E * jnp.log(jnp.sum(sums, axis=1, keepdims=True))
+    total = jnp.sum(row_lse) + jnp.sum(column_lse) - 2.0 * jnp.sum(diagonal)
     loss_value[0] = total * (float(np.log(2.0)) / (2.0 * batch_total))
 
     mine = lax.axis_index("dp")
@@ -224,7 +223,7 @@
     pair_weight = jnp.exp2(block - row_lse) + jnp.exp2(block - column_lse) - matched
     unit_grad = (scale_value * (0.5 / batch_total)) * jnp.dot(
         pair_weight.astype(jnp.bfloat16),
-        every[:, width : 2 * width],
+        other_all[...],
         preferred_element_type=jnp.float32,
     )
     unit_rows = unit[...]
@@ -239,38 +238,47 @@
     width = image_proj.shape[1]
     batch_total = row_count * len(order)
     f32, bf16 = jnp.float32, jnp.bfloat16
+    tiles = row_count * width // (8 * LANES)
     operands = (
-        image_pooled, text_pooled, image_gain, text_gain, image_proj, text_proj, logit_scale, pair_index
+        image_pooled, text_pooled, image_gain, text_gain, image_proj, text_proj, pair_index
     )
     sent, unit, side = pl.pallas_call(
         lambda *refs: embed_kernel(order, *refs),
         out_shape=(
-            jax.ShapeDtypeStruct((row_count, 2 * width + LANES), bf16),
+            jax.ShapeDtypeStruct((2 * tiles + 1, 8, LANES), bf16),
             jax.ShapeDtypeStruct((row_count, width), f32),
             jax.ShapeDtypeStruct((row_count, LANES), f32),
         ),
         in_specs=[pl.BlockSpec(memory_space=pltpu.HBM)] * len(operands),
         out_specs=[pl.BlockSpec(memory_space=pltpu.VMEM)] * 3,
         scratch_shapes=[pltpu.VMEM(x.shape, x.dtype) for x in operands]
-        + [pltpu.SemaphoreType.DMA((64,))],
+        + [pltpu.SemaphoreType.DMA((len(operands),))],
         compiler_params=pltpu.CompilerParams(vmem_limit_bytes=KERNEL_BYTES),
         name="embed",
-    )(*(x if x.shape == (1,) else pltpu.with_memory_space_constraint(x, pltpu.HBM) for x in operands))
+    )(*(pltpu.with_memory_space_constraint(x, pltpu.HBM) for x in operands))
     every = lax.all_gather(
         sent.astype(jnp.float16), "dp", axis=0, tiled=True, axis_index_groups=[order]
-    ).astype(bf16)
+    ).reshape(len(order), 2 * tiles + 1, 8, LANES)
+
+    def plain(blocks):
+        blocks = blocks.reshape(len(order), row_count // 8, width // LANES, 8, LANES)
+        return blocks.transpose(0, 1, 3, 2, 4).reshape(batch_total, width).astype(bf16)
+
+    own_all = plain(every[:, :tiles])
+    other_all = plain(every[:, tiles : 2 * tiles])
+    digits = every[:, 2 * tiles].astype(bf16)
     loss_value, embed_grad = pl.pallas_call(
         lambda *refs: score_kernel(order, *refs),
         out_shape=(
             jax.ShapeDtypeStruct((1,), f32),
             jax.ShapeDtypeStruct((1, row_count, width), f32),
         ),
-        in_specs=[pl.BlockSpec(memory_space=pltpu.VMEM)] * 3,
+        in_specs=[pl.BlockSpec(memory_space=pltpu.SMEM)] + [pl.BlockSpec(memory_space=pltpu.VMEM)] * 5,
         out_specs=[pl.BlockSpec(memory_space=pltpu.SMEM), pl.BlockSpec(memory_space=pltpu.VMEM)],
         scratch_shapes=[pltpu.VMEM((batch_total, batch_total), f32)],
         compiler_params=pltpu.CompilerParams(vmem_limit_bytes=KERNEL_BYTES),
         name="scores",
-    )(every, unit, side)
+    )(logit_scale, own_all, other_all, digits, unit, side)
     return (loss_value[0], embed_grad)
 
 
@@ -325,7 +333,8 @@
     def local(*args):
         batch_total = args[0].shape[0] * lax.axis_size("dp")
         small = 4 * batch_total * batch_total <= SCORE_BYTES
-        if small and batch_total % LANES == 0 and args[0].shape[0] % 8 == 0:
+        width = args[4].shape[1]
+        if small and batch_total % LANES == 0 and args[0].shape[0] % 8 == 0 and width % LANES == 0:
             return gather_both(order, *args)
         return gather_one(*args)
 

time: 31.5 us -> 29.8 us (0.946)
  Pallas kernels: 6.48 us -> 5.32 us
  blocking collectives: 23.3 us -> 22.6 us
    all_gather x1, blocking collectives: 23.3 us -> 22.6 us  [gather_both(): lax.all_gather(sent.astype(jnp.float16), 'dp', axis=0, tiled=True, axis_i...]
    pallas_call x1, Pallas kernels: 3.23 us -> 2.6 us  [gather_both(): pl.pallas_call(lambda *refs: embed_kernel(order, *refs), out_shape=(jax.S...]
    pallas_call x1, Pallas kernels: 3.24 us -> 2.72 us  [gather_both(): pl.pallas_call(lambda *refs: score_kernel(order, *refs), out_shape=(jax.S...]
where the time goes in v3:
time: 29.8 us; the launch traced here: 29.6 us
  blocking collectives  22.6 us (76%)
  Pallas kernels  5.32 us (18%)
  between operations  1.31 us (4%)
  other arithmetic  0.38 us (1%)
    all_gather x1, blocking collectives, gather_both(): lax.all_gather(sent.astype(jnp.float16), 'dp', axis=0, tiled=True, axis_i...  22.6 us
    pallas_call x1, Pallas kernels, gather_both(): pl.pallas_call(lambda *refs: score_kernel(order, *refs), out_shape=(jax.S...  2.72 us
    pallas_call x1, Pallas kernels, gather_both(): pl.pallas_call(lambda *refs: embed_kernel(order, *refs), out_shape=(jax.S...  2.6 us

profile of v3, /device:TPU:0, one launch (start us, length us, event | category | flops | bytes accessed | tf_op | source)
XLA Modules:
  0.0 29.6 jit_solution(5215332610045022111)
XLA Ops:
  0.6 2.6 %embed.1 = (bf16[61,8,128]{2,1,0:T(8,128)(2,1)S(1)}, f32[40,768]{1,0:T(8,128)S(1)}, f32[40,128]{1,0:T(8,128)S(1)}) custom-call(bf16[40,1024]{1,0:T(8,128)(2,1)} %refs_0_.2, bf16[40,768]{1,0:T(8,128)(2,1)} %refs_1_.1, f32[1024]{0:T(1024)} %refs_2_.1, f32[768]{0:T(1024)} %refs_3_.1, bf16[1024,768]{1,0:T(8,128)(2,1)} %refs_4_.1, bf16[768,768]{1,0:T(8,128)(2,1)} %refs_5_.1, ...), custom_call_target="tpu_custom_call" | custom-call | tf_op jit(solution)/shard_map/embed/pallas_call | solution.py:245
  3.3 22.6 %all-gather.1 = f16[976,8,128]{2,1,0:T(8,128)(2,1)S(1)} all-gather(f16[61,8,128]{2,1,0:T(8,128)(2,1)S(1)} %convert_element_type.26), channel_id=1, replica_groups={{0,1,4,5,8,9,12,13,14,15,10,11,6,7,2,3},{16,17,20,21,24,25,28,29,30,31,..., dimensions={0}, use_global_device_ids=true | all-gather | bytes 2123776 | tf_op jit(solution)/shard_map/all_gather | solution.py:259
  25.9 0.3 %slice_convert_fusion = (bf16[16,30,8,128]{3,2,1,0:T(8,128)(2,1)S(1)}, bf16[16,30,8,128]{3,2,1,0:T(8,128)(2,1)S(1)}) fusion(f16[16,61,8,128]{3,2,1,0:T(8,128)(2,1)S(1)} %bitcast.22), kind=kLoop, calls=%fused_computation | loop fusion | flops 983040 | bytes 3932160 | tf_op jit(solution)/shard_map/convert_element_type | solution.py:265
  26.9 2.7 %scores.1 = (f32[1]{0:T(128)}, f32[1,40,768]{2,1,0:T(8,128)}) custom-call(f32[1]{0:T(128)S(6)} %copy.15.refs_0_, bf16[640,768]{1,0:T(8,128)(2,1)S(1)} %bitcast.21, bf16[640,768]{1,0:T(8,128)(2,1)S(1)} %bitcast.20, bf16[16,8,128]{2,1,0:T(8,128)(2,1)S(1)} %fusion.1.refs_3_, f32[40,768]{1,0:T(8,128)S(1)} %get-tuple-element.8.refs_4_, ...), custom_call_target="tpu_custom_call" | custom-call | tf_op jit(solution)/shard_map/scores/pallas_call | solution.py:270
  (2 shorter events, 0.0 us)

commit v4 on v3

--- a/solution.py
+++ b/solution.py
@@ -13,6 +13,7 @@
 CHUNK = 256
 SCORE_BYTES = 2**22
 KERNEL_BYTES = 2**24
+NORM_COST = 925_000_000
 
 
 def closed_path(mesh):
@@ -79,43 +80,19 @@
     return table
 
 
-def embed_kernel(
+def norm_kernel(
     order,
     image_pooled,
     text_pooled,
     image_gain,
     text_gain,
-    image_proj,
-    text_proj,
     pair_index,
-    sent,
-    unit,
+    image_normed,
+    text_normed,
     side,
-    image_rows,
-    text_rows,
-    image_scale,
-    text_scale,
-    image_weight,
-    text_weight,
-    pair_row,
-    arrived,
 ):
-    row_count, width = unit.shape
-    moves = [
-        (pair_index, pair_row),
-        (image_pooled, image_rows),
-        (image_gain, image_scale),
-        (text_pooled, text_rows),
-        (text_gain, text_scale),
-        (image_proj, image_weight),
-        (text_proj, text_weight),
-    ]
-    copies = [pltpu.make_async_copy(a, b, arrived.at[i]) for i, (a, b) in enumerate(moves)]
-    for copy in copies:
-        copy.start()
-
-    copies[0].wait()
-    pairs = pair_row[...]
+    row_count = image_pooled.shape[0]
+    pairs = pair_index[...]
     places = pairs
     for here, sample in enumerate(order):
         inside = (pairs >= sample * row_count) & (pairs < (sample + 1) * row_count)
@@ -123,6 +100,16 @@
     square = (row_count, row_count)
     upright = lax.broadcasted_iota(jnp.int32, square, 0) == lax.broadcasted_iota(jnp.int32, square, 1)
     place = jnp.sum(jnp.where(upright, places.astype(jnp.float32), 0.0), axis=1, keepdims=True)
+    side[...] = jnp.broadcast_to(place, side.shape)
+    image_normed[...] = normalize(image_pooled[...], image_gain[...][None, :])
+    text_normed[...] = normalize(text_pooled[...], text_gain[...][None, :])
+
+
+def embed_kernel(
+    logit_scale, image_normed, text_normed, image_weight, text_weight, spots, sent, unit, side
+):
+    row_count, width = unit.shape
+    place = spots[:, 0:1]
     high = jnp.floor(place * (1.0 / LANES))
     across, down = width // LANES, row_count // 8
     for k in range(down):
@@ -132,26 +119,15 @@
         tile = jnp.where(lane == LOW_LANE + k, place[rows] - high[rows] * LANES, tile)
     sent[2 * across * down] = tile.astype(jnp.bfloat16)
 
-    copies[1].wait()
-    copies[2].wait()
-    image_normed = normalize(image_rows[...], image_scale[...][None, :])
-    copies[3].wait()
-    copies[4].wait()
-    text_normed = normalize(text_rows[...], text_scale[...][None, :])
-
-    def project(normed, weight):
-        return jnp.dot(normed, weight, preferred_element_type=jnp.float32)
-
-    def unitize_rows(embedded):
+    def unitize_rows(normed, weight):
+        embedded = jnp.dot(normed[...], weight[...], preferred_element_type=jnp.float32)
         squares = jnp.sum(embedded * embedded, axis=-1, keepdims=True) + 1e-06
         inverse = 1.0 / jnp.sqrt(squares)
         return embedded * inverse, inverse
 
     is_image = lax.axis_index("mod") == 0
-    copies[5].wait()
-    image_unit, image_inverse = unitize_rows(project(image_normed, image_weight[...]))
-    copies[6].wait()
-    text_unit, text_inverse = unitize_rows(project(text_normed, text_weight[...]))
+    image_unit, image_inverse = unitize_rows(image_normed, image_weight)
+    text_unit, text_inverse = unitize_rows(text_normed, text_weight)
     own = jnp.where(is_image, image_unit, text_unit)
     unit[...] = own
     other = jnp.where(is_image, text_unit, image_unit)
@@ -164,15 +140,23 @@
         {
             SIDE_INVERSE: jnp.where(is_image, image_inverse, text_inverse),
             SIDE_PLACE: place,
+            SIDE_SCALE: logit_scale[0],
         },
         (row_count, LANES),
     )
 
 
-def score_kernel(order, logit_scale, own_all, other_all, digits, unit, side, loss_value, embed_grad, scores):
+def fold_rows(block, reduce):
+    rows, lanes = block.shape
+    if rows % 64 == 0:
+        block = reduce(block.reshape(rows // 64, 64, lanes), axis=0)
+    return reduce(block, axis=0, keepdims=True)
+
+
+def score_kernel(order, own_all, other_all, digits, unit, side, loss_value, embed_grad, scores):
     row_count, width = unit.shape
     batch_total = own_all.shape[0]
-    scale_value = logit_scale[0]
+    scale_value = side[0:1, SIDE_SCALE : SIDE_SCALE + 1]
     factor = scale_value * LOG2_E
     column = lax.broadcasted_iota(jnp.int32, (1, batch_total), 1).astype(jnp.float32)
 
@@ -183,7 +167,7 @@
     )
     lanes = lax.broadcasted_iota(jnp.int32, (1, LANES), 1).astype(jnp.float32)
     row_tops = jnp.full((batch_total, LANES), -jnp.inf, jnp.float32)
-    diagonal = jnp.zeros((8, LANES), jnp.float32)
+    diagonal = jnp.zeros((batch_total, LANES), jnp.float32)
     column_lses = []
     for start in range(0, batch_total, CHUNK):
         count = min(CHUNK, batch_total - start)
@@ -194,23 +178,14 @@
             preferred_element_type=jnp.float32,
         )
         scores[:, start : start + count] = block
-        top = jnp.max(block, axis=0, keepdims=True)
-        total = jnp.sum(jnp.exp2(block - top), axis=0, keepdims=True)
+        top = fold_rows(block, jnp.max)
+        total = fold_rows(jnp.exp2(block - top), jnp.sum)
         column_lses.append(top + LOG2_E * jnp.log(total))
         for k in range(0, count, LANES):
             part = block[:, k : k + LANES]
             row_tops = jnp.maximum(row_tops, part)
-            hit = jnp.where(places == lanes + (start + k), part, 0.0)
-            diagonal = diagonal + jnp.sum(hit.reshape(batch_total // 8, 8, LANES), axis=0)
+            diagonal = jnp.where(places == lanes + (start + k), part, diagonal)
     column_lse = jnp.concatenate(column_lses, axis=1)
-    row_top = jnp.max(row_tops, axis=1, keepdims=True)
-    sums = jnp.zeros((batch_total, LANES), jnp.float32)
-    for start in range(0, batch_total, LANES):
-        sums = sums + jnp.exp2(scores[:, start : start + LANES] - row_top)
-    row_lse = row_top + LOG2_E * jnp.log(jnp.sum(sums, axis=1, keepdims=True))
-    total = jnp.sum(row_lse) + jnp.sum(column_lse) - 2.0 * jnp.sum(diagonal)
-    loss_value[0] = total * (float(np.log(2.0)) / (2.0 * batch_total))
-
     mine = lax.axis_index("dp")
     first = jnp.int32(0)
     for here, sample in enumerate(order):
@@ -230,6 +205,14 @@
     along = jnp.sum(unit_rows * unit_grad, axis=-1, keepdims=True)
     embed_grad[0] = (unit_grad - unit_rows * along) * side[:, SIDE_INVERSE : SIDE_INVERSE + 1]
 
+    row_top = jnp.max(row_tops, axis=1, keepdims=True)
+    sums = jnp.zeros((batch_total, LANES), jnp.float32)
+    for start in range(0, batch_total, LANES):
+        sums = sums + jnp.exp2(scores[:, start : start + LANES] - row_top)
+    row_lse = row_top + LOG2_E * jnp.log(jnp.sum(sums, axis=1, keepdims=True))
+    total = jnp.sum(fold_rows(row_lse, jnp.sum)) + jnp.sum(column_lse) - 2.0 * jnp.sum(fold_rows(diagonal, jnp.sum))
+    loss_value[0] = total * (float(np.log(2.0)) / (2.0 * batch_total))
+
 
 def gather_both(
     order, image_pooled, text_pooled, image_gain, text_gain, image_proj, text_proj, logit_scale, pair_index
@@ -239,23 +222,32 @@
     batch_total = row_count * len(order)
     f32, bf16 = jnp.float32, jnp.bfloat16
     tiles = row_count * width // (8 * LANES)
-    operands = (
-        image_pooled, text_pooled, image_gain, text_gain, image_proj, text_proj, pair_index
-    )
+    operands = (image_pooled, text_pooled, image_gain, text_gain, pair_index)
+    image_normed, text_normed, spots = pl.pallas_call(
+        lambda *refs: norm_kernel(order, *refs),
+        out_shape=(
+            jax.ShapeDtypeStruct(image_pooled.shape, bf16),
+            jax.ShapeDtypeStruct(text_pooled.shape, bf16),
+            jax.ShapeDtypeStruct((row_count, LANES), f32),
+        ),
+        in_specs=[pl.BlockSpec(memory_space=pltpu.VMEM)] * len(operands),
+        out_specs=[pl.BlockSpec(memory_space=pltpu.VMEM)] * 3,
+        compiler_params=pltpu.CompilerParams(vmem_limit_bytes=KERNEL_BYTES),
+        cost_estimate=pl.CostEstimate(flops=NORM_COST, bytes_accessed=4_000_000, transcendentals=0),
+        name="norm",
+    )(*(pltpu.with_memory_space_constraint(x, pltpu.HBM) for x in operands))
     sent, unit, side = pl.pallas_call(
-        lambda *refs: embed_kernel(order, *refs),
+        embed_kernel,
         out_shape=(
             jax.ShapeDtypeStruct((2 * tiles + 1, 8, LANES), bf16),
             jax.ShapeDtypeStruct((row_count, width), f32),
             jax.ShapeDtypeStruct((row_count, LANES), f32),
         ),
-        in_specs=[pl.BlockSpec(memory_space=pltpu.HBM)] * len(operands),
+        in_specs=[pl.BlockSpec(memory_space=pltpu.SMEM)] + [pl.BlockSpec(memory_space=pltpu.VMEM)] * 5,
         out_specs=[pl.BlockSpec(memory_space=pltpu.VMEM)] * 3,
-        scratch_shapes=[pltpu.VMEM(x.shape, x.dtype) for x in operands]
-        + [pltpu.SemaphoreType.DMA((len(operands),))],
         compiler_params=pltpu.CompilerParams(vmem_limit_bytes=KERNEL_BYTES),
         name="embed",
-    )(*(pltpu.with_memory_space_constraint(x, pltpu.HBM) for x in operands))
+    )(logit_scale, image_normed, text_normed, image_proj, text_proj, spots)
     every = lax.all_gather(
         sent.astype(jnp.float16), "dp", axis=0, tiled=True, axis_index_groups=[order]
     ).reshape(len(order), 2 * tiles + 1, 8, LANES)
@@ -273,12 +265,12 @@
             jax.ShapeDtypeStruct((1,), f32),
             jax.ShapeDtypeStruct((1, row_count, width), f32),
         ),
-        in_specs=[pl.BlockSpec(memory_space=pltpu.SMEM)] + [pl.BlockSpec(memory_space=pltpu.VMEM)] * 5,
+        in_specs=[pl.BlockSpec(memory_space=pltpu.VMEM)] * 5,
         out_specs=[pl.BlockSpec(memory_space=pltpu.SMEM), pl.BlockSpec(memory_space=pltpu.VMEM)],
         scratch_shapes=[pltpu.VMEM((batch_total, batch_total), f32)],
         compiler_params=pltpu.CompilerParams(vmem_limit_bytes=KERNEL_BYTES),
         name="scores",
-    )(logit_scale, own_all, other_all, digits, unit, side)
+    )(own_all, other_all, digits, unit, side)
     return (loss_value[0], embed_grad)
 
 

time: 29.8 us -> 29.2 us (0.980)
  Pallas kernels: 5.32 us -> 4.55 us
    pallas_call x1 -> x2, Pallas kernels: 2.6 us -> 1.9 us  [the longest x1 1.18 us: gather_both(): pl.pallas_call(lambda *refs: norm_kernel(order, *refs), out_shape=(jax.Sh...]
where the time goes in v4:
time: 29.2 us; the launch traced here: 29 us
  blocking collectives  22.6 us (77%)
  Pallas kernels  4.55 us (16%)
  between operations  1.49 us (5%)
  other arithmetic  0.37 us (1%)
    all_gather x1, blocking collectives, gather_both(): lax.all_gather(sent.astype(jnp.float16), 'dp', axis=0, tiled=True, axis_i...  22.6 us
    pallas_call x1, Pallas kernels, gather_both(): pl.pallas_call(lambda *refs: score_kernel(order, *refs), out_shape=(jax.S...  2.66 us
    pallas_call x1, Pallas kernels, gather_both(): pl.pallas_call(lambda *refs: norm_kernel(order, *refs), out_shape=(jax.Sh...  1.18 us
    pallas_call x1, Pallas kernels, gather_both(): pl.pallas_call(embed_kernel, out_shape=(jax.ShapeDtypeStruct((2 * tiles +...  0.72 us

profile of v4, /device:TPU:0, one launch (start us, length us, event | category | flops | bytes accessed | tf_op | source)
XLA Modules:
  0.0 29.0 jit_solution(16089719693962003463)
XLA Ops:
  0.6 0.0 copy-start.1
  0.6 0.0 copy-start
  1.4 1.2 %norm.1 = (bf16[40,1024]{1,0:T(8,128)(2,1)S(1)}, bf16[40,768]{1,0:T(8,128)(2,1)S(1)}, f32[40,128]{1,0:T(8,128)S(1)}) custom-call(bf16[40,1024]{1,0:T(8,128)(2,1)} %refs_0_.1, bf16[40,768]{1,0:T(8,128)(2,1)} %refs_1_.1, f32[1024]{0:T(1024)} %refs_2_.1, f32[768]{0:T(1024)} %refs_3_.1, s32[1,40]{1,0:T(1,128)} %refs_4_.1), custom_call_target="tpu_custom_call" | custom-call | flops 925000000 | bytes 4000000 | tf_op jit(solution)/shard_map/norm/pallas_call | solution.py:226
  2.6 0.0 copy-done.1
  2.6 0.0 copy-done
  2.7 0.7 %embed.1 = (bf16[61,8,128]{2,1,0:T(8,128)(2,1)S(1)}, f32[40,768]{1,0:T(8,128)S(1)}, f32[40,128]{1,0:T(8,128)S(1)}) custom-call(f32[1]{0:T(128)S(6)} %copy.15.logit_scale, bf16[40,1024]{1,0:T(8,128)(2,1)S(1)} %get-tuple-element.10.image_normed, bf16[40,768]{1,0:T(8,128)(2,1)S(1)} %get-tuple-element.11.text_normed, bf16[1024,768]{1,0:T(8,128)(2,1)S(1)} %copy-done, ...), custom_call_target="tpu_custom_call" | custom-call | tf_op jit(solution)/shard_map/embed/pallas_call | solution.py:239
  3.4 22.6 %all-gather.1 = f16[976,8,128]{2,1,0:T(8,128)(2,1)S(1)} all-gather(f16[61,8,128]{2,1,0:T(8,128)(2,1)S(1)} %convert_element_type.26), channel_id=1, replica_groups={{0,1,4,5,8,9,12,13,14,15,10,11,6,7,2,3},{16,17,20,21,24,25,28,29,30,31,..., dimensions={0}, use_global_device_ids=true | all-gather | bytes 2123776 | tf_op jit(solution)/shard_map/all_gather | solution.py:251
  26.0 0.3 %slice_convert_fusion = (bf16[16,30,8,128]{3,2,1,0:T(8,128)(2,1)S(1)}, bf16[16,30,8,128]{3,2,1,0:T(8,128)(2,1)S(1)}) fusion(f16[16,61,8,128]{3,2,1,0:T(8,128)(2,1)S(1)} %bitcast.23), kind=kLoop, calls=%fused_computation | loop fusion | flops 983040 | bytes 3932160 | tf_op jit(solution)/shard_map/convert_element_type | solution.py:257
  26.4 2.7 %scores.1 = (f32[1]{0:T(128)}, f32[1,40,768]{2,1,0:T(8,128)}) custom-call(bf16[640,768]{1,0:T(8,128)(2,1)S(1)} %bitcast.21, bf16[640,768]{1,0:T(8,128)(2,1)S(1)} %bitcast.20, bf16[16,8,128]{2,1,0:T(8,128)(2,1)S(1)} %fusion.1.refs_2_, f32[40,768]{1,0:T(8,128)S(1)} %get-tuple-element.14.refs_3_, f32[40,128]{1,0:T(8,128)S(1)} %get-tuple-element.15.refs_4_), custom_call_target="tpu_custom_call" | custom-call | tf_op jit(solution)/shard_map/scores/pallas_call | solution.py:262
  (2 shorter events, 0.0 us)
Async XLA Ops:
  0.6 2.0 %copy-start.1 = (bf16[768,768]{1,0:T(8,128)(2,1)S(1)}, bf16[768,768]{1,0:T(8,128)(2,1)}, u32[]{:S(2)}) copy-start(bf16[768,768]{1,0:T(8,128)(2,1)} %text_weight.1) | copy-start | bytes 3538948
  0.6 2.0 %copy-start = (bf16[1024,768]{1,0:T(8,128)(2,1)S(1)}, bf16[1024,768]{1,0:T(8,128)(2,1)}, u32[]{:S(2)}) copy-start(bf16[1024,768]{1,0:T(8,128)(2,1)} %image_weight.1) | copy-start | bytes 4718596

commit v5 on v4

--- a/solution.py
+++ b/solution.py
@@ -13,7 +13,8 @@
 CHUNK = 256
 SCORE_BYTES = 2**22
 KERNEL_BYTES = 2**24
-NORM_COST = 925_000_000
+NORM_COST = 100_000_000
+SCALE_COST = 800_000_000
 
 
 def closed_path(mesh):
@@ -80,8 +81,13 @@
     return table
 
 
+def scale_kernel(logit_scale, spread):
+    spread[...] = jnp.full(spread.shape, logit_scale[0], jnp.float32)
+
+
 def norm_kernel(
     order,
+    spread,
     image_pooled,
     text_pooled,
     image_gain,
@@ -100,16 +106,17 @@
     square = (row_count, row_count)
     upright = lax.broadcasted_iota(jnp.int32, square, 0) == lax.broadcasted_iota(jnp.int32, square, 1)
     place = jnp.sum(jnp.where(upright, places.astype(jnp.float32), 0.0), axis=1, keepdims=True)
-    side[...] = jnp.broadcast_to(place, side.shape)
+    shape = side.shape
+    side[...] = lane_table({SIDE_PLACE: place, SIDE_SCALE: spread[0:1, 0:1]}, shape)
     image_normed[...] = normalize(image_pooled[...], image_gain[...][None, :])
     text_normed[...] = normalize(text_pooled[...], text_gain[...][None, :])
 
 
 def embed_kernel(
-    logit_scale, image_normed, text_normed, image_weight, text_weight, spots, sent, unit, side
+    image_normed, text_normed, image_weight, text_weight, spots, sent, unit, side
 ):
     row_count, width = unit.shape
-    place = spots[:, 0:1]
+    place = spots[:, SIDE_PLACE : SIDE_PLACE + 1]
     high = jnp.floor(place * (1.0 / LANES))
     across, down = width // LANES, row_count // 8
     for k in range(down):
@@ -140,7 +147,7 @@
         {
             SIDE_INVERSE: jnp.where(is_image, image_inverse, text_inverse),
             SIDE_PLACE: place,
-            SIDE_SCALE: logit_scale[0],
+            SIDE_SCALE: spots[:, SIDE_SCALE : SIDE_SCALE + 1],
         },
         (row_count, LANES),
     )
@@ -223,6 +230,15 @@
     f32, bf16 = jnp.float32, jnp.bfloat16
     tiles = row_count * width // (8 * LANES)
     operands = (image_pooled, text_pooled, image_gain, text_gain, pair_index)
+    spread = pl.pallas_call(
+        scale_kernel,
+        out_shape=jax.ShapeDtypeStruct((8, LANES), f32),
+        in_specs=[pl.BlockSpec(memory_space=pltpu.SMEM)],
+        out_specs=pl.BlockSpec(memory_space=pltpu.VMEM),
+        compiler_params=pltpu.CompilerParams(vmem_limit_bytes=KERNEL_BYTES),
+        cost_estimate=pl.CostEstimate(flops=SCALE_COST, bytes_accessed=4_000_000, transcendentals=0),
+        name="scale",
+    )(logit_scale)
     image_normed, text_normed, spots = pl.pallas_call(
         lambda *refs: norm_kernel(order, *refs),
         out_shape=(
@@ -230,12 +246,12 @@
             jax.ShapeDtypeStruct(text_pooled.shape, bf16),
             jax.ShapeDtypeStruct((row_count, LANES), f32),
         ),
-        in_specs=[pl.BlockSpec(memory_space=pltpu.VMEM)] * len(operands),
+        in_specs=[pl.BlockSpec(memory_space=pltpu.VMEM)] * (1 + len(operands)),
         out_specs=[pl.BlockSpec(memory_space=pltpu.VMEM)] * 3,
         compiler_params=pltpu.CompilerParams(vmem_limit_bytes=KERNEL_BYTES),
         cost_estimate=pl.CostEstimate(flops=NORM_COST, bytes_accessed=4_000_000, transcendentals=0),
         name="norm",
-    )(*(pltpu.with_memory_space_constraint(x, pltpu.HBM) for x in operands))
+    )(spread, *operands)
     sent, unit, side = pl.pallas_call(
         embed_kernel,
         out_shape=(
@@ -243,11 +259,11 @@
             jax.ShapeDtypeStruct((row_count, width), f32),
             jax.ShapeDtypeStruct((row_count, LANES), f32),
         ),
-        in_specs=[pl.BlockSpec(memory_space=pltpu.SMEM)] + [pl.BlockSpec(memory_space=pltpu.VMEM)] * 5,
+        in_specs=[pl.BlockSpec(memory_space=pltpu.VMEM)] * 5,
         out_specs=[pl.BlockSpec(memory_space=pltpu.VMEM)] * 3,
         compiler_params=pltpu.CompilerParams(vmem_limit_bytes=KERNEL_BYTES),
         name="embed",
-    )(logit_scale, image_normed, text_normed, image_proj, text_proj, spots)
+    )(image_normed, text_normed, image_proj, text_proj, spots)
     every = lax.all_gather(
         sent.astype(jnp.float16), "dp", axis=0, tiled=True, axis_index_groups=[order]
     ).reshape(len(order), 2 * tiles + 1, 8, LANES)

time: 29.2 us -> 29.1 us (level)
  Pallas kernels: 4.55 us -> 3.58 us
  local copies, waits for them, and re-layouts: 0.01 us -> 0.8 us
    pallas_call x1, Pallas kernels: 1.18 us -> 0.21 us  [gather_both(): pl.pallas_call(lambda *refs: norm_kernel(order, *refs), out_shape=(jax.Sh...]
    unnamed x4 -> x14, local copies, waits for them, and re-layouts: 0.01 us -> 0.8 us
where the time goes in v5:
time: 29.1 us; the launch traced here: 28.9 us
  blocking collectives  22.6 us (78%)
  Pallas kernels  3.58 us (12%)
  between operations  1.54 us (5%)
  local copies, waits for them, and re-layouts  0.8 us (3%)
  other arithmetic  0.37 us (1%)
    all_gather x1, blocking collectives, gather_both(): lax.all_gather(sent.astype(jnp.float16), 'dp', axis=0, tiled=True, axis_i...  22.6 us
    pallas_call x1, Pallas kernels, gather_both(): pl.pallas_call(lambda *refs: score_kernel(order, *refs), out_shape=(jax.S...  2.66 us
    unnamed x14, local copies, waits for them, and re-layouts  0.8 us
    pallas_call x1, Pallas kernels, gather_both(): pl.pallas_call(embed_kernel, out_shape=(jax.ShapeDtypeStruct((2 * tiles +...  0.71 us

profile of v5, /device:TPU:0, one launch (start us, length us, event | category | flops | bytes accessed | tf_op | source)
XLA Modules:
  0.0 28.9 jit_solution(7104081472506360416)
XLA Ops:
  0.6 0.0 copy-start.6
  0.6 0.0 copy-start.1
  0.7 0.0 copy-start
  0.7 0.0 copy-start.5
  0.7 0.0 copy-start.4
  0.7 0.0 copy-start.3
  0.7 0.0 copy-start.2
  1.5 0.0 copy-done.6
  1.5 0.0 copy-done.5
  1.5 0.0 copy-done.4
  1.5 0.2 copy-done.3
  1.7 0.1 copy-done.2
  1.8 0.2 norm.1
  2.0 0.0 copy-done.1
  2.0 0.5 %copy-done = bf16[1024,768]{1,0:T(8,128)(2,1)S(1)} copy-done((bf16[1024,768]{1,0:T(8,128)(2,1)S(1)}, bf16[1024,768]{1,0:T(8,128)(2,1)}, u32[]{:S(2)}) %copy-start) | copy-done | bytes 1572888
  2.5 0.7 %embed.1 = (bf16[61,8,128]{2,1,0:T(8,128)(2,1)S(1)}, f32[40,768]{1,0:T(8,128)S(1)}, f32[40,128]{1,0:T(8,128)S(1)}) custom-call(bf16[40,1024]{1,0:T(8,128)(2,1)S(1)} %get-tuple-element.10.image_normed, bf16[40,768]{1,0:T(8,128)(2,1)S(1)} %get-tuple-element.11.text_normed, bf16[1024,768]{1,0:T(8,128)(2,1)S(1)} %copy-done, bf16[768,768]{1,0:T(8,128)(2,1)S(1)} %copy-done.1, ...), custom_call_target="tpu_custom_call" | custom-call | tf_op jit(solution)/shard_map/embed/pallas_call | solution.py:255
  3.3 22.6 %all-gather.1 = f16[976,8,128]{2,1,0:T(8,128)(2,1)S(1)} all-gather(f16[61,8,128]{2,1,0:T(8,128)(2,1)S(1)} %convert_element_type.26), channel_id=1, replica_groups={{0,1,4,5,8,9,12,13,14,15,10,11,6,7,2,3},{16,17,20,21,24,25,28,29,30,31,..., dimensions={0}, use_global_device_ids=true | all-gather | bytes 2123776 | tf_op jit(solution)/shard_map/all_gather | solution.py:267
  25.9 0.3 %slice_convert_fusion = (bf16[16,30,8,128]{3,2,1,0:T(8,128)(2,1)S(1)}, bf16[16,30,8,128]{3,2,1,0:T(8,128)(2,1)S(1)}) fusion(f16[16,61,8,128]{3,2,1,0:T(8,128)(2,1)S(1)} %bitcast.23), kind=kLoop, calls=%fused_computation | loop fusion | flops 983040 | bytes 3932160 | tf_op jit(solution)/shard_map/convert_element_type | solution.py:273
  26.2 2.7 %scores.1 = (f32[1]{0:T(128)}, f32[1,40,768]{2,1,0:T(8,128)}) custom-call(bf16[640,768]{1,0:T(8,128)(2,1)S(1)} %bitcast.21, bf16[640,768]{1,0:T(8,128)(2,1)S(1)} %bitcast.20, bf16[16,8,128]{2,1,0:T(8,128)(2,1)S(1)} %fusion.1.refs_2_, f32[40,768]{1,0:T(8,128)S(1)} %get-tuple-element.14.refs_3_, f32[40,128]{1,0:T(8,128)S(1)} %get-tuple-element.15.refs_4_), custom_call_target="tpu_custom_call" | custom-call | tf_op jit(solution)/shard_map/scores/pallas_call | solution.py:278
  (3 shorter events, 0.0 us)
Async XLA Ops:
  0.6 0.9 %copy-start.6 = (s32[1,40]{1,0:T(1,128)S(1)}, s32[1,40]{1,0:T(1,128)}, u32[]{:S(2)}) copy-start(s32[1,40]{1,0:T(1,128)} %refs_5_.1) | copy-start | bytes 484
  0.6 1.4 %copy-start.1 = (bf16[768,768]{1,0:T(8,128)(2,1)S(1)}, bf16[768,768]{1,0:T(8,128)(2,1)}, u32[]{:S(2)}) copy-start(bf16[768,768]{1,0:T(8,128)(2,1)} %text_weight.1) | copy-start | bytes 3538948
  0.7 1.9 %copy-start = (bf16[1024,768]{1,0:T(8,128)(2,1)S(1)}, bf16[1024,768]{1,0:T(8,128)(2,1)}, u32[]{:S(2)}) copy-start(bf16[1024,768]{1,0:T(8,128)(2,1)} %image_weight.1) | copy-start | bytes 4718596
  0.7 0.9 %copy-start.5 = (f32[768]{0:T(1024)S(1)}, f32[768]{0:T(1024)}, u32[]{:S(2)}) copy-start(f32[768]{0:T(1024)} %refs_4_.1) | copy-start | bytes 9220
  0.7 0.9 %copy-start.4 = (f32[1024]{0:T(1024)S(1)}, f32[1024]{0:T(1024)}, u32[]{:S(2)}) copy-start(f32[1024]{0:T(1024)} %refs_3_.1) | copy-start | bytes 12292
  0.7 1.0 %copy-start.3 = (bf16[40,768]{1,0:T(8,128)(2,1)S(1)}, bf16[40,768]{1,0:T(8,128)(2,1)}, u32[]{:S(2)}) copy-start(bf16[40,768]{1,0:T(8,128)(2,1)} %refs_2_.1) | copy-start | bytes 184324
  0.7 1.1 %copy-start.2 = (bf16[40,1024]{1,0:T(8,128)(2,1)S(1)}, bf16[40,1024]{1,0:T(8,128)(2,1)}, u32[]{:S(2)}) copy-start(bf16[40,1024]{1,0:T(8,128)(2,1)} %refs_1_.1) | copy-start | bytes 245764

commit v6 on v5

--- a/solution.py
+++ b/solution.py
@@ -13,7 +13,8 @@
 CHUNK = 256
 SCORE_BYTES = 2**22
 KERNEL_BYTES = 2**24
-NORM_COST = 100_000_000
+NORM_COST = 1_000_000
+IMAGE_COST = 1_000_000
 SCALE_COST = 800_000_000
 
 
@@ -112,9 +113,19 @@
     text_normed[...] = normalize(text_pooled[...], text_gain[...][None, :])
 
 
-def embed_kernel(
-    image_normed, text_normed, image_weight, text_weight, spots, sent, unit, side
-):
+def unitize_rows(normed, weight):
+    embedded = jnp.dot(normed, weight, preferred_element_type=jnp.float32)
+    squares = jnp.sum(embedded * embedded, axis=-1, keepdims=True) + 1e-06
+    inverse = 1.0 / jnp.sqrt(squares)
+    return embedded * inverse, inverse
+
+
+def image_kernel(normed, weight, unit, inverse):
+    unit[...], scaling = unitize_rows(normed[...], weight[...])
+    inverse[...] = jnp.broadcast_to(scaling, inverse.shape)
+
+
+def embed_kernel(image_unit, image_inverse, text_normed, text_weight, spots, sent, unit, side):
     row_count, width = unit.shape
     place = spots[:, SIDE_PLACE : SIDE_PLACE + 1]
     high = jnp.floor(place * (1.0 / LANES))
@@ -126,18 +137,11 @@
         tile = jnp.where(lane == LOW_LANE + k, place[rows] - high[rows] * LANES, tile)
     sent[2 * across * down] = tile.astype(jnp.bfloat16)
 
-    def unitize_rows(normed, weight):
-        embedded = jnp.dot(normed[...], weight[...], preferred_element_type=jnp.float32)
-        squares = jnp.sum(embedded * embedded, axis=-1, keepdims=True) + 1e-06
-        inverse = 1.0 / jnp.sqrt(squares)
-        return embedded * inverse, inverse
-
     is_image = lax.axis_index("mod") == 0
-    image_unit, image_inverse = unitize_rows(image_normed, image_weight)
-    text_unit, text_inverse = unitize_rows(text_normed, text_weight)
-    own = jnp.where(is_image, image_unit, text_unit)
+    text_unit, text_inverse = unitize_rows(text_normed[...], text_weight[...])
+    own = jnp.where(is_image, image_unit[...], text_unit)
     unit[...] = own
-    other = jnp.where(is_image, text_unit, image_unit)
+    other = jnp.where(is_image, text_unit, image_unit[...])
     for base, rows in ((0, own), (across * down, other)):
         for i in range(down):
             for k in range(across):
@@ -145,7 +149,7 @@
                 sent[base + i * across + k] = tile.astype(jnp.bfloat16)
     side[...] = lane_table(
         {
-            SIDE_INVERSE: jnp.where(is_image, image_inverse, text_inverse),
+            SIDE_INVERSE: jnp.where(is_image, image_inverse[:, 0:1], text_inverse),
             SIDE_PLACE: place,
             SIDE_SCALE: spots[:, SIDE_SCALE : SIDE_SCALE + 1],
         },
@@ -252,6 +256,18 @@
         cost_estimate=pl.CostEstimate(flops=NORM_COST, bytes_accessed=4_000_000, transcendentals=0),
         name="norm",
     )(spread, *operands)
+    image_unit, image_inverse = pl.pallas_call(
+        image_kernel,
+        out_shape=(
+            jax.ShapeDtypeStruct((row_count, width), f32),
+            jax.ShapeDtypeStruct((row_count, LANES), f32),
+        ),
+        in_specs=[pl.BlockSpec(memory_space=pltpu.VMEM)] * 2,
+        out_specs=[pl.BlockSpec(memory_space=pltpu.VMEM)] * 2,
+        compiler_params=pltpu.CompilerParams(vmem_limit_bytes=KERNEL_BYTES),
+        cost_estimate=pl.CostEstimate(flops=IMAGE_COST, bytes_accessed=4_000_000, transcendentals=0),
+        name="image",
+    )(image_normed, image_proj)
     sent, unit, side = pl.pallas_call(
         embed_kernel,
         out_shape=(
@@ -263,7 +279,7 @@
         out_specs=[pl.BlockSpec(memory_space=pltpu.VMEM)] * 3,
         compiler_params=pltpu.CompilerParams(vmem_limit_bytes=KERNEL_BYTES),
         name="embed",
-    )(image_normed, text_normed, image_proj, text_proj, spots)
+    )(image_unit, image_inverse, text_normed, text_proj, spots)
     every = lax.all_gather(
         sent.astype(jnp.float16), "dp", axis=0, tiled=True, axis_index_groups=[order]
     ).reshape(len(order), 2 * tiles + 1, 8, LANES)

time: 29.1 us -> 29.2 us (level)
    pallas_call x0 -> x1, Pallas kernels: none -> 0.47 us  [gather_both(): pl.pallas_call(image_kernel, out_shape=(jax.ShapeDtypeStruct((row_count,...]
where the time goes in v6:
time: 29.2 us; the launch traced here: 29 us
  blocking collectives  22.6 us (77%)
  Pallas kernels  3.85 us (13%)
  between operations  1.52 us (5%)
  local copies, waits for them, and re-layouts  0.66 us (2%)
  other arithmetic  0.37 us (1%)
    all_gather x1, blocking collectives, gather_both(): lax.all_gather(sent.astype(jnp.float16), 'dp', axis=0, tiled=True, axis_i...  22.6 us
    pallas_call x1, Pallas kernels, gather_both(): pl.pallas_call(lambda *refs: score_kernel(order, *refs), out_shape=(jax.S...  2.65 us
    unnamed x14, local copies, waits for them, and re-layouts  0.66 us

profile of v6, /device:TPU:0, one launch (start us, length us, event | category | flops | bytes accessed | tf_op | source)
XLA Modules:
  0.0 29.0 jit_solution(3422048457416951953)
XLA Ops:
  0.6 0.0 copy-start.6
  0.6 0.0 copy-start
  0.7 0.0 copy-start.5
  0.7 0.0 copy-start.4
  0.7 0.0 copy-start.3
  0.7 0.0 copy-start.2
  1.5 0.0 copy-start.1
  1.5 0.0 copy-done.6
  1.5 0.0 copy-done.5
  1.5 0.0 copy-done.4
  1.5 0.1 copy-done.3
  1.6 0.1 copy-done.2
  1.7 0.2 norm.1
  2.0 0.2 copy-done
  2.2 0.5 %image.1 = (f32[40,768]{1,0:T(8,128)S(1)}, f32[40,128]{1,0:T(8,128)S(1)}) custom-call(bf16[40,1024]{1,0:T(8,128)(2,1)S(1)} %get-tuple-element.12.normed, bf16[1024,768]{1,0:T(8,128)(2,1)S(1)} %copy-done), custom_call_target="tpu_custom_call" | custom-call | flops 1000000 | bytes 4000000 | tf_op jit(solution)/shard_map/image/pallas_call | solution.py:259
  2.7 0.2 copy-done.1
  2.8 0.5 %embed.1 = (bf16[61,8,128]{2,1,0:T(8,128)(2,1)S(1)}, f32[40,768]{1,0:T(8,128)S(1)}, f32[40,128]{1,0:T(8,128)S(1)}) custom-call(f32[40,768]{1,0:T(8,128)S(1)} %get-tuple-element.13.image_unit, f32[40,128]{1,0:T(8,128)S(1)} %get-tuple-element.14.image_inverse, bf16[40,768]{1,0:T(8,128)(2,1)S(1)} %get-tuple-element.15.text_normed, ...), custom_call_target="tpu_custom_call" | custom-call | tf_op jit(solution)/shard_map/embed/pallas_call | solution.py:271
  3.4 22.6 %all-gather.1 = f16[976,8,128]{2,1,0:T(8,128)(2,1)S(1)} all-gather(f16[61,8,128]{2,1,0:T(8,128)(2,1)S(1)} %convert_element_type.26), channel_id=1, replica_groups={{0,1,4,5,8,9,12,13,14,15,10,11,6,7,2,3},{16,17,20,21,24,25,28,29,30,31,..., dimensions={0}, use_global_device_ids=true | all-gather | bytes 2123776 | tf_op jit(solution)/shard_map/all_gather | solution.py:283
  26.0 0.3 %slice_convert_fusion = (bf16[16,30,8,128]{3,2,1,0:T(8,128)(2,1)S(1)}, bf16[16,30,8,128]{3,2,1,0:T(8,128)(2,1)S(1)}) fusion(f16[16,61,8,128]{3,2,1,0:T(8,128)(2,1)S(1)} %bitcast.23), kind=kLoop, calls=%fused_computation | loop fusion | flops 983040 | bytes 3932160 | tf_op jit(solution)/shard_map/convert_element_type | solution.py:289
  26.3 2.6 %scores.1 = (f32[1]{0:T(128)}, f32[1,40,768]{2,1,0:T(8,128)}) custom-call(bf16[640,768]{1,0:T(8,128)(2,1)S(1)} %bitcast.21, bf16[640,768]{1,0:T(8,128)(2,1)S(1)} %bitcast.20, bf16[16,8,128]{2,1,0:T(8,128)(2,1)S(1)} %fusion.1.refs_2_, f32[40,768]{1,0:T(8,128)S(1)} %get-tuple-element.18.refs_3_, f32[40,128]{1,0:T(8,128)S(1)} %get-tuple-element.19.refs_4_), custom_call_target="tpu_custom_call" | custom-call | tf_op jit(solution)/shard_map/scores/pallas_call | solution.py:294
  (3 shorter events, 0.0 us)
Async XLA Ops:
  0.6 0.8 %copy-start.6 = (s32[1,40]{1,0:T(1,128)S(1)}, s32[1,40]{1,0:T(1,128)}, u32[]{:S(2)}) copy-start(s32[1,40]{1,0:T(1,128)} %refs_5_.1) | copy-start | bytes 484
  0.6 1.5 %copy-start = (bf16[1024,768]{1,0:T(8,128)(2,1)S(1)}, bf16[1024,768]{1,0:T(8,128)(2,1)}, u32[]{:S(2)}) copy-start(bf16[1024,768]{1,0:T(8,128)(2,1)} %weight.1) | copy-start | bytes 4718596
  0.7 0.8 %copy-start.5 = (f32[768]{0:T(1024)S(1)}, f32[768]{0:T(1024)}, u32[]{:S(2)}) copy-start(f32[768]{0:T(1024)} %refs_4_.1) | copy-start | bytes 9220
  0.7 0.8 %copy-start.4 = (f32[1024]{0:T(1024)S(1)}, f32[1024]{0:T(1024)}, u32[]{:S(2)}) copy-start(f32[1024]{0:T(1024)} %refs_3_.1) | copy-start | bytes 12292
  0.7 1.0 %copy-start.3 = (bf16[40,768]{1,0:T(8,128)(2,1)S(1)}, bf16[40,768]{1,0:T(8,128)(2,1)}, u32[]{:S(2)}) copy-start(bf16[40,768]{1,0:T(8,128)(2,1)} %refs_2_.1) | copy-start | bytes 184324
  0.7 1.1 %copy-start.2 = (bf16[40,1024]{1,0:T(8,128)(2,1)S(1)}, bf16[40,1024]{1,0:T(8,128)(2,1)}, u32[]{:S(2)}) copy-start(bf16[40,1024]{1,0:T(8,128)(2,1)} %refs_1_.1) | copy-start | bytes 245764
  1.5 1.4 %copy-start.1 = (bf16[768,768]{1,0:T(8,128)(2,1)S(1)}, bf16[768,768]{1,0:T(8,128)(2,1)}, u32[]{:S(2)}) copy-start(bf16[768,768]{1,0:T(8,128)(2,1)} %text_weight.1) | copy-start | bytes 3538948
